TPU v7x, 16 devices: a whole 2x2x2 slice. The times are simulated.
16 devices in a mesh: ep: 16 (over z, y, x, core).
Axes of the slice: x: 2, y: 2, z: 2, core: 2. Of those that a mesh axis runs over, the one named last changes fastest.
Arguments:
- x_tokens: bfloat16 [32768, 1024], P('ep')
- w_router: bfloat16 [1024, 32], replicated
- w_gate: bfloat16 [32, 1024, 512], P('ep')
- w_up: bfloat16 [32, 1024, 512], P('ep')
- w_down: bfloat16 [32, 512, 1024], P('ep')
- topk_idx: int32 [32768, 8], P('ep')
- dy_tokens: bfloat16 [32768, 1024], P('ep')
Outputs:
- output 1: bfloat16 [32768, 1024], P('ep')
- output 2: float32 [], replicated
- output 3: bfloat16 [32768, 1024], P('ep')
- output 4: float32 [1024, 32], replicated
- output 5: float32 [32, 1024, 512], P('ep')
- output 6: float32 [32, 1024, 512], P('ep')
- output 7: float32 [32, 512, 1024], P('ep')
All inputs are finite; a program needn't handle non-finite values.
Results may differ from a plain program's by a relative error of at most 0.00538827.
Values are sent between devices in bfloat16 or wider.
A program may use at most 1 GiB of HBM per device.

v0:
```python
import jax
import jax.numpy as jnp
from jax import lax
from jax.sharding import PartitionSpec as P

AUX_COEF = 0.001


def route_slots(idx_dev, n_exp, capacity):
    tok_count, top_k = idx_dev.shape
    choice_mask = idx_dev[:, :, None] == jnp.arange(n_exp, dtype=jnp.int32)
    expert_hot = jnp.sum(choice_mask.astype(jnp.int32), axis=1)
    earlier = jnp.cumsum(expert_hot, axis=0) - expert_hot
    position = jnp.take_along_axis(earlier, idx_dev, axis=1)
    slot_ids = jnp.where(position < capacity, idx_dev * capacity + position, n_exp * capacity)
    pair_ids = jnp.arange(tok_count * top_k, dtype=jnp.int32)
    empty_fill = jnp.full((n_exp * capacity,), tok_count * top_k, jnp.int32)
    pair_of_slot = empty_fill.at[slot_ids.reshape(-1)].set(pair_ids, mode="drop")
    return slot_ids, pair_of_slot, choice_mask, expert_hot


def solution(mesh):
    n_dev = mesh.shape["ep"]

    def local_block(x_loc, w_router, wg_loc, wu_loc, wd_loc, idx_loc, dy_loc):
        tok_count, model_dim = x_loc.shape
        top_k = idx_loc.shape[1]
        n_exp = w_router.shape[1]
        loc_exp = wg_loc.shape[0]
        capacity = (5 * tok_count * top_k + 4 * n_exp - 1) // (4 * n_exp)
        n_total = tok_count * n_dev
        logits = jnp.dot(x_loc, w_router, preferred_element_type=jnp.float32)
        router_prob = jax.nn.softmax(logits, axis=-1)
        pick_prob = jnp.take_along_axis(router_prob, idx_loc, axis=1)
        pick_sum = jnp.sum(pick_prob, axis=1, keepdims=True)
        gate_f32 = pick_prob / pick_sum
        gate_bf = gate_f32.astype(jnp.bfloat16)
        slot_ids, pair_of_slot, choice_mask, expert_hot = route_slots(idx_loc, n_exp, capacity)
        tok_of_slot = pair_of_slot // top_k
        buf_shape = (n_dev, loc_exp, capacity, model_dim)

        send_x = jnp.take(x_loc, tok_of_slot, axis=0, mode="fill", fill_value=0).reshape(buf_shape)
        recv_x = lax.all_to_all(send_x, "ep", 0, 1)
        gate_pre = jnp.einsum("egcd,edf->egcf", recv_x, wg_loc, preferred_element_type=jnp.float32)
        up_pre = jnp.einsum("egcd,edf->egcf", recv_x, wu_loc, preferred_element_type=jnp.float32)
        act_gate = jax.nn.silu(gate_pre)
        hidden = (act_gate * up_pre).astype(jnp.bfloat16)
        out_slot = jnp.einsum("egcf,efd->egcd", hidden, wd_loc, preferred_element_type=jnp.float32).astype(jnp.bfloat16)
        back_out = lax.all_to_all(out_slot, "ep", 1, 0).reshape(n_exp * capacity, model_dim)
        out_tok = jnp.take(back_out, slot_ids, axis=0, mode="fill", fill_value=0)
        y_loc = jnp.einsum("tk,tkd->td", gate_bf, out_tok, preferred_element_type=jnp.float32).astype(jnp.bfloat16)

        load_stats = jnp.concatenate([jnp.sum(expert_hot, axis=0).astype(jnp.float32), jnp.sum(router_prob, axis=0)])
        load_stats = lax.psum(load_stats, "ep")
        load_frac = load_stats[:n_exp] / (n_total * top_k)
        mean_prob = load_stats[n_exp:] / n_total
        aux_loss = AUX_COEF * n_exp * jnp.sum(load_frac * mean_prob)

        gate_slot = jnp.take(gate_bf.reshape(-1), pair_of_slot, mode="fill", fill_value=0)
        dy_slot = jnp.take(dy_loc, tok_of_slot, axis=0, mode="fill", fill_value=0)
        send_do = (gate_slot[:, None] * dy_slot).reshape(buf_shape)
        recv_do = lax.all_to_all(send_do, "ep", 0, 1)
        dw_down = jnp.einsum("egcf,egcd->efd", hidden, recv_do, preferred_element_type=jnp.float32)
        d_hidden = jnp.einsum("egcd,efd->egcf", recv_do, wd_loc, preferred_element_type=jnp.float32).astype(jnp.bfloat16).astype(jnp.float32)
        sigmoid_g = jax.nn.sigmoid(gate_pre)
        d_gate_pre = (d_hidden * up_pre * sigmoid_g * (1.0 + gate_pre * (1.0 - sigmoid_g))).astype(jnp.bfloat16)
        d_up_pre = (d_hidden * act_gate).astype(jnp.bfloat16)
        dw_gate = jnp.einsum("egcd,egcf->edf", recv_x, d_gate_pre, preferred_element_type=jnp.float32)
        dw_up = jnp.einsum("egcd,egcf->edf", recv_x, d_up_pre, preferred_element_type=jnp.float32)
        dx_slot = (jnp.einsum("egcf,edf->egcd", d_gate_pre, wg_loc, preferred_element_type=jnp.float32)
                   + jnp.einsum("egcf,edf->egcd", d_up_pre, wu_loc, preferred_element_type=jnp.float32)).astype(jnp.bfloat16)
        back_dx = lax.all_to_all(dx_slot, "ep", 1, 0).reshape(n_exp * capacity, model_dim)
        dx_tok = jnp.take(back_dx, slot_ids, axis=0, mode="fill", fill_value=0)
        dx_expert = jnp.sum(dx_tok, axis=1, dtype=jnp.float32)

        d_gate = jnp.einsum("tkd,td->tk", out_tok, dy_loc, preferred_element_type=jnp.float32)
        d_pick = (d_gate - jnp.sum(d_gate * gate_f32, axis=1, keepdims=True)) / pick_sum
        d_prob = jnp.sum(jnp.where(choice_mask, d_pick[:, :, None], 0.0), axis=1) + AUX_COEF * n_exp * load_frac / n_total
        d_logit = router_prob * (d_prob - jnp.sum(router_prob * d_prob, axis=1, keepdims=True))
        d_logit_bf = d_logit.astype(jnp.bfloat16)
        dw_router = lax.psum(jnp.einsum("td,te->de", x_loc, d_logit_bf, preferred_element_type=jnp.float32), "ep")
        dx_loc = (dx_expert + jnp.einsum("te,de->td", d_logit_bf, w_router, preferred_element_type=jnp.float32)).astype(jnp.bfloat16)
        return y_loc, aux_loss, dx_loc, dw_router, dw_gate, dw_up, dw_down

    tok_spec = P("ep")
    return jax.shard_map(
        local_block,
        mesh=mesh,
        in_specs=(tok_spec, P(), tok_spec, tok_spec, tok_spec, tok_spec, tok_spec),
        out_specs=(tok_spec, P(), tok_spec, P(), tok_spec, tok_spec, tok_spec),
        check_vma=False,
    )
```

profile of v0, /device:TPU:0, one launch (start us, length us, event | category | flops | bytes accessed | tf_op | source)
XLA Modules:
  0.0 3706.6 jit_solution(1351103399701241724)
XLA Ops:
  7.2 1.0 bitcast_or_fusion
  8.2 1.8 convert_reduce_fusion.1
  10.0 9.1 reduce-window.6
  19.2 0.2 copy.109
  19.9 0.3 copy.76
  20.3 0.5 reshape.148
  20.8 130.6 %gather_fusion.2 = s32[16384]{0:T(1024)S(1)} fusion(s32[2048,32]{0,1:T(8,128)S(1)} %fusion.46, s32[16384]{0:T(1024)S(1)} %reshape.148), kind=kCustom, calls=%fused_computation.6 | custom fusion | bytes 262144 | tf_op jit(solution)/shard_map/jit(take_along_axis)/gather | solution.py:14
  151.3 0.6 reshape.157
  151.9 0.3 copy.80
  152.2 1.5 compare_and_fusion.1
  153.7 0.3 copy.82
  154.1 0.5 reshape.107
  154.7 60.4 %scatter_custom_fusion = s32[20480]{0:T(1024)S(1)} fusion(s32[16384]{0:T(1024)S(1)} %bitcast.150, s32[16384]{0:T(1024)S(1)} %iota.7, s32[]{:T(128)} %constant.76.clone.1), kind=kCustom, calls=%fused_computation.96 | custom fusion | bytes 81924 | tf_op jit(solution)/shard_map/scatter | solution.py:18
  215.1 0.7 compare_and_fusion
  215.8 0.7 fusion.51
  216.5 3.5 fusion.62
  220.1 0.7 fusion.60
  220.9 130.5 %gather_fusion.1 = f32[16384]{0:T(1024)S(1)} fusion(f32[2048,32]{0,1:T(8,128)S(1)} %get-tuple-element.12, s32[16384]{0:T(1024)S(1)} %reshape.148), kind=kCustom, calls=%fused_computation.5 | custom fusion | bytes 262144 | tf_op jit(solution)/shard_map/jit(take_along_axis)/gather | solution.py:34
  351.4 0.6 reshape.151
  352.0 0.3 copy.77
  352.3 0.6 copy-done.8
  352.9 0.6 copy-done.19
  353.6 0.3 copy.88
  353.8 0.5 convert_element_type.52
  354.4 126.3 %gather_fusion = bf16[20480]{0:T(1024)(128)(2,1)S(1)} fusion(bf16[16384]{0:T(1024)(128)(2,1)S(1)} %convert_element_type.52, s32[20480]{0:T(1024)} %get-tuple-element.19), kind=kCustom, calls=%fused_computation.4 | custom fusion | bytes 163840 | tf_op jit(solution)/shard_map/jit(_take)/gather | solution.py:59
  480.6 0.6 and_select_fusion
  481.3 102.7 %gather_fusion.3 = bf16[20480,1024]{1,0:T(8,128)(2,1)} fusion(bf16[2048,1024]{1,0:T(8,128)(2,1)} %param.11, s32[20480]{0:T(1024)S(1)} %copy-done.10), kind=kCustom, calls=%fused_computation.clone | custom fusion | bytes 83968000 | tf_op jit(solution)/shard_map/jit(_take)/gather | solution.py:42
  584.0 102.7 %gather_fusion.5 = bf16[20480,1024]{1,0:T(8,128)(2,1)} fusion(bf16[2048,1024]{1,0:T(8,128)(2,1)} %param.17, s32[20480]{0:T(1024)S(1)} %copy-done.10), kind=kCustom, calls=%fused_computation.2.clone | custom fusion | bytes 83968000 | tf_op jit(solution)/shard_map/jit(_take)/gather | solution.py:60
  686.6 54.1 %select_multiply_fusion = (bf16[20480,1024]{1,0:T(8,128)(2,1)}, bf16[20480,1024]{1,0:T(8,128)(2,1)}) fusion(bf16[20480,1024]{1,0:T(8,128)(2,1)} %gather_fusion.5, pred[20480]{0:T(1024)(128)(4,1)S(1)} %copy-done.21, bf16[20480]{0:T(1024)(128)(2,1)S(1)} %copy-done.18, bf16[20480,1024]{1,0:T(8,128)(2,1)} %gather_fusion.3), kind=kLoop, calls=%fused_computation.25 | loop fusion | flops 62914560 | bytes 167833600 | tf_op jit(solution)/shard_map/mul | solution.py:61
  740.8 464.7 %all_to_all.60 = bf16[16,2,1,640,1024]{4,3,1,2,0:T(8,128)(2,1)} all-to-all(bf16[16,2,1,640,1024]{4,3,1,2,0:T(8,128)(2,1)} %bitcast.142), channel_id=1, replica_groups=mesh['ep'=16] {'ep'}, dimensions={0} | all-to-all | bytes 83886080 | tf_op jit(solution)/shard_map/all_to_all | solution.py:62
  1205.5 5.2 all-to-all-start
  1210.7 29.8 fusion.26
  1240.6 470.1 %all-to-all-done = bf16[16,2,1,640,1024]{4,3,1,2,0:T(8,128)(2,1)} async-done(((bf16[16,2,1,640,1024]{4,3,1,2,0:T(8,128)(2,1)}), bf16[16,2,1,640,1024]{4,3,1,2,0:T(8,128)(2,1)}, u32[]{:S(2)}, u32[]{:S(2)}) %all-to-all-start) | async-done | bytes 41943072 | tf_op jit(solution)/shard_map/all_to_all | solution.py:43
  1710.7 36.1 fusion.11
  1746.7 65.8 %fusion.2 = (bf16[2,16,640,512]{3,2,1,0:T(8,128)(2,1)}, bf16[2,16,640,512]{3,2,1,0:T(8,128)(2,1)}, bf16[2,16,640,512]{3,2,1,0:T(8,128)(2,1)}) fusion(bf16[2,16,640,512]{3,2,1,0:T(8,128)(2,1)} %fusion.26, f32[2,16,640,512]{3,2,1,0:T(8,128)} %fusion.11, bf16[2,1024,512]{2,1,0:T(8,128)(2,1)S(1)} %copy-done, bf16[16,2,1,640,1024]{4,3,1,2,0:T(8,128)(2,1)} %all-to-all-done), kind=kOutput, calls=%fused_computation.14 | convolution fusion | flops 21642608640 | bytes 169869312 | tf_op jit(solution)/shard_map/egcd,edf->egcf/dot_general | solution.py:45
  1812.5 30.5 convert_bitcast_fusion
  1843.0 28.4 copy.85
  1871.4 5.4 all-to-all-start.1
  1876.7 39.7 %fusion.41 = f32[2,16,640,1024]{3,2,1,0:T(8,128)} fusion(bf16[2,16,640,512]{3,2,1,0:T(8,128)(2,1)} %get-tuple-element.16, bf16[2,1024,512]{2,1,0:T(8,128)(2,1)} %param.13), kind=kOutput, calls=%fused_computation.56 | convolution fusion | flops 21474836480 | bytes 106954752 | tf_op jit(solution)/shard_map/egcf,edf->egcd/dot_general | solution.py:70
  1916.4 48.6 %fusion.4 = bf16[1,2,16,640,1024]{4,3,2,1,0:T(8,128)(2,1)} fusion(f32[2,16,640,1024]{3,2,1,0:T(8,128)} %fusion.41, bf16[2,16,640,512]{3,2,1,0:T(8,128)(2,1)} %get-tuple-element.18, bf16[2,1024,512]{2,1,0:T(8,128)(2,1)S(1)} %copy-done), kind=kOutput, calls=%fused_computation.16 | convolution fusion | flops 21516779520 | bytes 148897792 | tf_op jit(solution)/shard_map/egcf,edf->egcd/dot_general | solution.py:71
  1965.0 28.3 copy.91
  1993.4 383.7 %all-to-all-done.1 = bf16[1,2,16,640,1024]{4,3,1,0,2:T(8,128)(2,1)} async-done(((bf16[1,2,16,640,1024]{4,3,1,0,2:T(8,128)(2,1)}), bf16[1,2,16,640,1024]{4,3,1,0,2:T(8,128)(2,1)}, u32[]{:S(2)}, u32[]{:S(2)}) %all-to-all-start.1) | async-done | bytes 41943072 | tf_op jit(solution)/shard_map/all_to_all | solution.py:49
  2377.1 5.0 all-to-all-start.3
  2382.2 1.1 copy.81
  2383.3 0.3 copy.86
  2383.6 0.5 reshape.182
  2384.1 2.0 copy.99
  2386.2 522.9 %psum.14 = f32[64]{0:T(128)S(1)} all-reduce(f32[64]{0:T(128)S(1)} %pad_maximum_fusion), channel_id=1, replica_groups=mesh['ep'=16] {'ep'}, use_global_device_ids=true, to_apply=%region_9.12 | all-reduce | flops 64 | bytes 512 | tf_op jit(solution)/shard_map/psum | solution.py:54
  2909.1 1.1 slice_multiply_fusion
  2910.9 0.6 broadcast_clamp_fusion.1
  2911.5 30.2 fusion.36
  2941.7 30.1 fusion.30
  2971.8 30.4 fusion.33
  3002.2 299.9 %gather_fusion.4 = bf16[16384,1024]{1,0:T(8,128)(2,1)} fusion(bf16[20480,1024]{1,0:T(8,128)(2,1)} %bitcast.23, s32[16384]{0:T(1024)S(1)} %copy-done.3), kind=kCustom, calls=%fused_computation.1.clone | custom fusion | bytes 67174400 | tf_op jit(solution)/shard_map/jit(_take)/gather | solution.py:50
  3302.2 27.2 fusion.22
  3329.4 2.2 copy.102
  3331.7 0.2 select_reduce_fusion
  3332.2 3.7 convolution_bitcast_fusion
  3335.9 19.8 fusion.23
  3355.7 300.4 %gather_fusion.6 = bf16[16384,1024]{1,0:T(8,128)(2,1)} fusion(bf16[20480,1024]{1,0:T(8,128)(2,1)} %bitcast.37, s32[16384]{0:T(1024)S(1)} %copy-done.3), kind=kCustom, calls=%fused_computation.3.clone | custom fusion | bytes 67174400 | tf_op jit(solution)/shard_map/jit(_take)/gather | solution.py:73
  3656.1 26.8 convert_reduce_fusion
  3682.9 6.7 add_convert_fusion.1
  3689.5 7.1 copy.150
  3696.6 1.6 copy.152
  (71 shorter events, 1.3 us)
Async XLA Ops:
  7.2 1739.5 %copy-start = (bf16[2,1024,512]{2,1,0:T(8,128)(2,1)S(1)}, bf16[2,1024,512]{2,1,0:T(8,128)(2,1)}, u32[]{:S(2)}) copy-start(bf16[2,1024,512]{2,1,0:T(8,128)(2,1)} %param.14) | copy-start | bytes 6291460
  153.7 67.1 %copy-start.11 = (s32[2048,8]{0,1:T(8,128)}, s32[2048,8]{0,1:T(8,128)S(1)}, u32[]{:S(2)}) copy-start(s32[2048,8]{0,1:T(8,128)S(1)} %get-tuple-element.14) | copy-start | bytes 196612
  215.1 5.0 copy-start.4
  220.9 130.6 %copy-start.1 = (f32[2048,32]{0,1:T(8,128)}, f32[2048,32]{0,1:T(8,128)S(1)}, u32[]{:S(2)}) copy-start(f32[2048,32]{0,1:T(8,128)S(1)} %get-tuple-element.12) | copy-start | bytes 786436
  220.9 131.4 %copy-start.16 = (pred[2048,8]{0,1:T(8,128)(4,1)S(1)}, pred[2048,8]{0,1:T(8,128)(4,1)}, u32[]{:S(2)}) copy-start(pred[2048,8]{0,1:T(8,128)(4,1)} %get-tuple-element.15) | copy-start | bytes 49156
  352.3 0.6 copy-start.8
  352.9 0.6 copy-start.19
  353.5 127.1 %copy-start.13 = (bf16[2048,8]{0,1:T(8,128)(2,1)}, bf16[2048,8]{0,1:T(8,128)(2,1)S(1)}, u32[]{:S(2)}) copy-start(bf16[2048,8]{0,1:T(8,128)(2,1)S(1)} %fusion.57) | copy-start | bytes 98308
  354.3 126.3 %copy-start.5 = (s32[20480]{0:T(1024)S(1)}, s32[20480]{0:T(1024)}, u32[]{:S(2)}) copy-start(s32[20480]{0:T(1024)} %copy-done.4) | copy-start | bytes 245764
  354.3 126.9 %copy-start.10 = (s32[20480]{0:T(1024)S(1)}, s32[20480]{0:T(1024)}, u32[]{:S(2)}) copy-start(s32[20480]{0:T(1024)} %get-tuple-element.20) | copy-start | bytes 245764
  584.0 102.7 %copy-start.18 = (bf16[20480]{0:T(1024)(128)(2,1)S(1)}, bf16[20480]{0:T(1024)(128)(2,1)}, u32[]{:S(2)}) copy-start(bf16[20480]{0:T(1024)(128)(2,1)} %and_select_fusion) | copy-start | bytes 122884
  584.0 102.7 %copy-start.21 = (pred[20480]{0:T(1024)(128)(4,1)S(1)}, pred[20480]{0:T(1024)(128)(4,1)}, u32[]{:S(2)}) copy-start(pred[20480]{0:T(1024)(128)(4,1)} %compare_and_fusion) | copy-start | bytes 61444
  1205.5 505.2 %all-to-all-start = ((bf16[16,2,1,640,1024]{4,3,1,2,0:T(8,128)(2,1)}), bf16[16,2,1,640,1024]{4,3,1,2,0:T(8,128)(2,1)}, u32[]{:S(2)}, u32[]{:S(2)}) async-start(bf16[16,2,1,640,1024]{4,3,1,2,0:T(8,128)(2,1)} %bitcast.141), calls=%async_computation | async-start | bytes 83886080 | tf_op jit(solution)/shard_map/all_to_all | solution.py:43
  1871.4 505.7 %all-to-all-start.1 = ((bf16[1,2,16,640,1024]{4,3,1,0,2:T(8,128)(2,1)}), bf16[1,2,16,640,1024]{4,3,1,0,2:T(8,128)(2,1)}, u32[]{:S(2)}, u32[]{:S(2)}) async-start(bf16[1,2,16,640,1024]{4,3,1,0,2:T(8,128)(2,1)} %copy.85), calls=%async_computation.1 | async-start | bytes 83886080 | tf_op jit(solution)/shard_map/all_to_all | solution.py:49
  1993.3 388.8 %copy-start.24 = (s32[32]{0:T(128)S(1)}, s32[32]{0:T(128)}, u32[]{:S(2)}) copy-start(s32[32]{0:T(128)} %get-tuple-element.9) | copy-start | bytes 388
  1993.3 388.9 %copy-start.22 = (pred[2048,8]{0,1:T(8,128)(4,1)S(1)}, pred[2048,8]{0,1:T(8,128)(4,1)}, u32[]{:S(2)}) copy-start(pred[2048,8]{0,1:T(8,128)(4,1)} %get-tuple-element.13) | copy-start | bytes 49156
  1993.4 389.9 %copy-start.12 = (s32[2048,8]{0,1:T(8,128)S(1)}, s32[2048,8]{0,1:T(8,128)}, u32[]{:S(2)}) copy-start(s32[2048,8]{0,1:T(8,128)} %copy-done.11) | copy-start | bytes 196612
  1993.4 390.8 %copy-start.14 = (bf16[2048,8]{0,1:T(8,128)(2,1)S(1)}, bf16[2048,8]{0,1:T(8,128)(2,1)}, u32[]{:S(2)}) copy-start(bf16[2048,8]{0,1:T(8,128)(2,1)} %copy-done.13) | copy-start | bytes 98308
  1993.4 392.7 %copy-start.25 = (f32[32]{0:T(128)S(1)}, f32[32]{0:T(128)}, u32[]{:S(2)}) copy-start(f32[32]{0:T(128)} %get-tuple-element.11) | copy-start | bytes 388
  2377.1 978.6 %all-to-all-start.3 = ((bf16[1,2,16,640,1024]{4,3,1,0,2:T(8,128)(2,1)}), bf16[1,2,16,640,1024]{4,3,1,0,2:T(8,128)(2,1)}, u32[]{:S(2)}, u32[]{:S(2)}) async-start(bf16[1,2,16,640,1024]{4,3,1,0,2:T(8,128)(2,1)} %copy.91), calls=%async_computation.3 | async-start | bytes 83886080 | tf_op jit(solution)/shard_map/all_to_all | solution.py:72
  2382.1 1314.5 %all-reduce.2.cloned.1.call-start = ((), (), s32[]{:S(2)}) async-start(), calls=%async_computation.4 | async-start | bytes 262144 | tf_op jit(solution)/shard_map/psum | solution.py:81
  2971.8 30.4 copy-start.3
  3002.2 299.9 %copy-start.6 = (pred[2048,8]{1,0:T(8,128)(4,1)S(1)}, pred[2048,8]{1,0:T(8,128)(4,1)}, u32[]{:S(2)}) copy-start(pred[2048,8]{1,0:T(8,128)(4,1)} %copy.81) | copy-start | bytes 49156
  3302.2 29.4 copy-start.9
  3302.2 29.4 copy-start.17
  3302.2 29.5 copy-start.20
  3302.2 29.5 copy-start.7
  3302.2 29.8 copy-start.2
  3302.2 29.8 copy-start.23
  3656.1 26.8 copy-start.15
Sparse Core Ops, SparseCore 0:
  3336.0 66.3 all-reduce.1
where the time goes:
time: 3730 us; the launch traced here: 3710 us
  local copies, waits for them, and re-layouts  1330 us (36%)
  blocking collectives  988 us (26%)
  waiting for transfers between devices  854 us (23%)
  matrix products  402 us (11%)
  other arithmetic  100 us (3%)
    psum x1, blocking collectives, local_block(): load_stats = lax.psum(load_stats, 'ep')  523 us
    all_to_all x1, waiting for transfers between devices, local_block(): recv_x = lax.all_to_all(send_x, 'ep', 0, 1)  470 us
    all_to_all x1, blocking collectives, local_block(): recv_do = lax.all_to_all(send_do, 'ep', 0, 1)  465 us
    all_to_all x1, waiting for transfers between devices, local_block(): lax.all_to_all(out_slot, 'ep', 1, 0).reshape(n_exp * capacity, model_dim)  384 us
    gather x1, local copies, waits for them, and re-layouts, local_block(): dx_tok = jnp.take(back_dx, slot_ids, axis=0, mode='fill', fill_value=0)  300 us
    gather x1, local copies, waits for them, and re-layouts, local_block(): out_tok = jnp.take(back_out, slot_ids, axis=0, mode='fill', fill_value=0)  300 us
    gather x5, local copies, waits for them, and re-layouts, local_block(): pick_prob = jnp.take_along_axis(router_prob, idx_loc, axis=1)  132 us
    gather x3, local copies, waits for them, and re-layouts, route_slots(): position = jnp.take_along_axis(earlier, idx_dev, axis=1)  131 us
  transfers between devices with their start and end apart: 4, of which 2 were waited for; matrix products, arithmetic and copies ran while one was open for 25% of the time, Pallas kernels for 0%

commit v1 on v0

v1 whole, which is shorter than its diff:
```python
import functools

import jax
import jax.numpy as jnp
from jax import lax
from jax.experimental import pallas as pl
from jax.experimental.pallas import tpu as pltpu
from jax.sharding import PartitionSpec as P

AUX_COEF = 0.001
SEG = 512
WIN = 192
TILE = 640
F32, BF16 = jnp.float32, jnp.bfloat16


def mm(a, b, ca=1, cb=0):
    return lax.dot_general(a, b, (((ca,), (cb,)), ((), ())), preferred_element_type=F32)


def window(cnt_ref, row, b):
    start = (cnt_ref[row, b] // 16) * 16
    return pl.multiple_of(start, 16), jnp.maximum((cnt_ref[row, b + 1] - start + WIN - 1) // WIN, 1)


def hot_rows(pos_ref, b, start):
    pos = pos_ref[0, :, b * SEG:(b + 1) * SEG] - start
    return lax.broadcasted_iota(jnp.int32, (WIN, SEG), 0) == pos


def gather_rows(cnt_ref, row, pos_ref, w_ref, x_ref, dy_ref, xs, dys, ds, n_seg, n_rows):
    end = 0
    for b in range(n_seg):
        first, n_win = window(cnt_ref, row, b)

        def step(c, _, b=b, first=first):
            start = pl.multiple_of(first + c * WIN, 16)
            hot = hot_rows(pos_ref, b, start)
            sel = hot.astype(F32).astype(BF16)
            tok = slice(b * SEG, (b + 1) * SEG)
            w_col = jnp.sum(jnp.where(hot, w_ref[0, :, tok], 0.0), axis=1, keepdims=True)
            x_new = mm(sel, x_ref[tok, :])
            dy_new = mm(sel, dy_ref[tok, :])
            d_new = w_col * dy_new
            outs = [(xs, x_new), (ds, d_new)] + ([(dys, dy_new)] if dys is not None else [])
            for ref, new in outs:
                new = new.astype(BF16)
                ref[pl.ds(start + 16, WIN - 16), :] = new[16:]
                if b == 0:
                    ref[pl.ds(start, 16), :] = new[:16]
                else:
                    old = ref[pl.ds(start, 16), :].astype(F32)
                    keep = jnp.where(c == 0, 1.0, 0.0)
                    ref[pl.ds(start, 16), :] = (jnp.where(keep > 0, old, 0.0) + new[:16].astype(F32)).astype(BF16)
            return 0

        step(0, 0)
        lax.fori_loop(1, n_win, step, 0)
        end = first + n_win * WIN

    def clear(i, _):
        at = pl.multiple_of(i * 16, 16)
        zero = jnp.zeros((16, xs.shape[1]), BF16)
        xs[pl.ds(at, 16), :] = zero
        ds[pl.ds(at, 16), :] = zero
        if dys is not None:
            dys[pl.ds(at, 16), :] = zero
        return 0

    lax.fori_loop(end // 16, n_rows // 16, clear, 0)


def slot_grads(x, d, wg, wu, wd):
    g = mm(x, wg)
    u = mm(x, wu)
    s = jax.nn.sigmoid(g)
    act = g * s
    h = (act * u).astype(BF16)
    dh = mm(d, wd, 1, 1).astype(BF16).astype(F32)
    dg = (dh * u * s * (1.0 + g * (1.0 - s))).astype(BF16)
    du = (dh * act).astype(BF16)
    return h, dg, du


def token_kernel(first, cnt_ref, pos_ref, w_ref, x_ref, dy_ref, wg_ref, wu_ref, wd_ref, y_in, dx_in,
                 y_out, dx_out, a_out, xs, dys, ds, os, dxs, y_acc, dx_acc, sems):
    i = pl.program_id(0)
    n_seg = x_ref.shape[0] // SEG

    @pl.when(i == 0)
    def _():
        if first:
            y_acc[...] = jnp.zeros_like(y_acc)
            dx_acc[...] = jnp.zeros_like(dx_acc)
        else:
            loads = [pltpu.make_async_copy(y_in, y_acc, sems.at[0]), pltpu.make_async_copy(dx_in, dx_acc, sems.at[1])]
            for copy in loads:
                copy.start()
            for copy in loads:
                copy.wait()
        os[...] = jnp.zeros_like(os)
        dxs[...] = jnp.zeros_like(dxs)

    gather_rows(cnt_ref, i, pos_ref, w_ref, x_ref, dy_ref, xs, dys, ds, n_seg, TILE)
    h, dg, du = slot_grads(xs[:TILE, :], ds[:TILE, :], wg_ref[0], wu_ref[0], wd_ref[0])
    o = mm(h, wd_ref[0]).astype(BF16)
    os[:TILE, :] = o
    dxs[:TILE, :] = (mm(dg, wg_ref[0], 1, 1) + mm(du, wu_ref[0], 1, 1)).astype(BF16)

    for b in range(n_seg):
        start0, n_win = window(cnt_ref, i, b)
        tok = slice(b * SEG, (b + 1) * SEG)

        def step(c, a_row, b=b, start0=start0, tok=tok):
            start = pl.multiple_of(start0 + c * WIN, 16)
            hot = hot_rows(pos_ref, b, start)
            sel = hot.astype(F32)
            sel_w = jnp.where(hot, w_ref[0, :, tok], 0.0).astype(BF16)
            o_win = os[pl.ds(start, WIN), :]
            y_acc[tok, :] += mm(sel_w, o_win, 0, 0)
            dx_acc[tok, :] += mm(sel.astype(BF16), dxs[pl.ds(start, WIN), :], 0, 0)
            a_col = jnp.sum(o_win.astype(F32) * dys[pl.ds(start, WIN), :].astype(F32), axis=1, keepdims=True)
            return a_row + jnp.sum(jnp.where(hot, a_col, 0.0), axis=0, keepdims=True)

        a_row = step(0, jnp.zeros((1, SEG), F32))
        a_out[0, :, tok] = lax.fori_loop(1, n_win, step, a_row)

    @pl.when(i == pl.num_programs(0) - 1)
    def _():
        stores = [pltpu.make_async_copy(y_acc, y_out, sems.at[0]), pltpu.make_async_copy(dx_acc, dx_out, sems.at[1])]
        for copy in stores:
            copy.start()
        for copy in stores:
            copy.wait()


def token_side(first, cnt, pos, w, x, dy, wg, wu, wd, y_in, dx_in):
    n_exp, _, tok_count = pos.shape
    dim, ff = wg.shape[1:]
    whole = lambda shape: pl.BlockSpec(shape, lambda i, c: (0,) * len(shape), pipeline_mode=pl.Buffered(1))
    per_exp = lambda shape: pl.BlockSpec((1,) + shape, lambda i, c: (i, 0, 0))
    any_spec = pl.BlockSpec(memory_space=pl.ANY)
    acc_shape = jax.ShapeDtypeStruct((tok_count, dim), F32)
    return pl.pallas_call(
        functools.partial(token_kernel, first),
        grid_spec=pltpu.PrefetchScalarGridSpec(
            num_scalar_prefetch=1,
            grid=(n_exp,),
            in_specs=[per_exp((1, tok_count)), per_exp((1, tok_count)), whole((tok_count, dim)), whole((tok_count, dim)),
                      per_exp((dim, ff)), per_exp((dim, ff)), per_exp((ff, dim)), any_spec, any_spec],
            out_specs=[any_spec, any_spec, per_exp((1, tok_count))],
            scratch_shapes=[pltpu.VMEM((TILE + WIN, dim), BF16)] * 5 + [pltpu.VMEM((tok_count, dim), F32)] * 2
            + [pltpu.SemaphoreType.DMA((2,))],
        ),
        out_shape=[acc_shape, acc_shape, jax.ShapeDtypeStruct((n_exp, 1, tok_count), F32)],
        input_output_aliases={} if first else {8: 0, 9: 1},
        compiler_params=pltpu.CompilerParams(dimension_semantics=("arbitrary",), vmem_limit_bytes=67000000),
        cost_estimate=pl.CostEstimate(flops=n_exp * 12 * 640 * dim * ff * 2, bytes_accessed=100 << 20, transcendentals=0),
        name="token_side",
    )(cnt, pos, w, x, dy, wg, wu, wd, y_in, dx_in)


def owner_kernel(first, cnt_ref, pos_ref, w_ref, x_ref, dy_ref, wg_ref, wu_ref, wd_ref, ag_in, au_in, ad_in,
                 ag_out, au_out, ad_out, xs, ds, ag, au, ad, sems):
    g, e = pl.program_id(0), pl.program_id(1)
    n_grp, n_exp = pl.num_programs(0), pl.num_programs(1)
    n_seg = x_ref.shape[0] // SEG
    row = g * n_exp + e
    accs = (ag, au, ad)

    @pl.when((g == 0) & (e == 0))
    def _():
        if first:
            for acc in accs:
                acc[...] = jnp.zeros_like(acc)
        else:
            loads = [pltpu.make_async_copy(src, acc, sems.at[k]) for k, (src, acc) in enumerate(zip((ag_in, au_in, ad_in), accs))]
            for copy in loads:
                copy.start()
            for copy in loads:
                copy.wait()

    n_tile = (cnt_ref[row, n_seg] + TILE - 1) // TILE
    gather_rows(cnt_ref, row, pos_ref, w_ref, x_ref, dy_ref, xs, None, ds, n_seg, n_tile * TILE)

    def tile(t, _):
        at = pl.multiple_of(t * TILE, 16)
        x, d = xs[pl.ds(at, TILE), :], ds[pl.ds(at, TILE), :]
        h, dg, du = slot_grads(x, d, wg_ref[0], wu_ref[0], wd_ref[0])
        ad[e] += mm(h, d, 0, 0)
        ag[e] += mm(x, dg, 0, 0)
        au[e] += mm(x, du, 0, 0)
        return 0

    lax.fori_loop(0, n_tile, tile, 0)

    @pl.when((g == n_grp - 1) & (e == n_exp - 1))
    def _():
        stores = [pltpu.make_async_copy(acc, dst, sems.at[k]) for k, (dst, acc) in enumerate(zip((ag_out, au_out, ad_out), accs))]
        for copy in stores:
            copy.start()
        for copy in stores:
            copy.wait()


def owner_side(first, cnt, pos, w, x, dy, wg, wu, wd, accs):
    n_exp, dim, ff = wg.shape
    grp = pos.shape[2]
    n_grp = x.shape[0] // grp
    per_row = pl.BlockSpec((1, 1, grp), lambda g, e, c: (g * n_exp + e, 0, 0))
    per_grp = pl.BlockSpec((grp, dim), lambda g, e, c: (g, 0))
    per_exp = lambda shape: pl.BlockSpec((1,) + shape, lambda g, e, c: (e, 0, 0))
    any_spec = pl.BlockSpec(memory_space=pl.ANY)
    rows = -(-grp // TILE) * TILE + WIN
    return pl.pallas_call(
        functools.partial(owner_kernel, first),
        grid_spec=pltpu.PrefetchScalarGridSpec(
            num_scalar_prefetch=1,
            grid=(n_grp, n_exp),
            in_specs=[per_row, per_row, per_grp, per_grp, per_exp((dim, ff)), per_exp((dim, ff)), per_exp((ff, dim))]
            + [any_spec] * 3,
            out_specs=[any_spec] * 3,
            scratch_shapes=[pltpu.VMEM((rows, dim), BF16)] * 2
            + [pltpu.VMEM((n_exp, dim, ff), F32)] * 2 + [pltpu.VMEM((n_exp, ff, dim), F32), pltpu.SemaphoreType.DMA((3,))],
        ),
        out_shape=[jax.ShapeDtypeStruct(a.shape, F32) for a in accs],
        input_output_aliases={} if first else {8: 0, 9: 1, 10: 2},
        compiler_params=pltpu.CompilerParams(dimension_semantics=("arbitrary", "arbitrary"), vmem_limit_bytes=67000000),
        cost_estimate=pl.CostEstimate(flops=n_grp * n_exp * 12 * 640 * dim * ff * 2, bytes_accessed=100 << 20, transcendentals=0),
        name="owner_side",
    )(cnt, pos, w, x, dy, wg, wu, wd, *accs)


def running_count(hot):
    rows, width = hot.shape
    blocks = hot.reshape(rows, width // 256, 256)
    upper = (jnp.arange(256)[:, None] < jnp.arange(256)[None, :]).astype(BF16)
    inside = jnp.einsum("rbi,ij->rbj", blocks.astype(BF16), upper, preferred_element_type=F32)
    total = jnp.sum(blocks, axis=2)
    n_blk = width // 256
    before = jnp.sum(jnp.where(jnp.arange(n_blk)[:, None] < jnp.arange(n_blk + 1)[None, :], total[:, :, None], 0.0), axis=1)
    return (inside + before[:, :-1, None]).reshape(rows, width), before[:, ::SEG // 256]


def solution(mesh):
    n_dev = mesh.shape["ep"]

    def local_block(x_loc, w_router, wg_loc, wu_loc, wd_loc, idx_loc, dy_loc):
        tok_count, dim = x_loc.shape
        top_k = idx_loc.shape[1]
        n_exp = w_router.shape[1]
        loc_exp = wg_loc.shape[0]
        capacity = (5 * tok_count * top_k + 4 * n_exp - 1) // (4 * n_exp)
        n_total = tok_count * n_dev
        n_chunk = 2
        span = tok_count // n_chunk
        gather = lambda a: lax.all_gather(a, "ep", axis=0, tiled=True)

        w_all = [gather(a) for a in (wg_loc, wu_loc, wd_loc)]
        tok_all = [[gather(a[c * span:(c + 1) * span]) for a in (x_loc, dy_loc)] for c in range(n_chunk)]

        idx_t = idx_loc.T
        exp_id = jnp.arange(n_exp, dtype=jnp.int32)[:, None]
        hot = exp_id == idx_t[0:1]
        for k in range(1, top_k):
            hot = hot | (exp_id == idx_t[k:k + 1])
        logits = lax.dot_general(w_router, x_loc, (((0,), (1,)), ((), ())), preferred_element_type=F32)
        prob = jax.nn.softmax(logits, axis=0)
        pick_sum = jnp.sum(jnp.where(hot, prob, 0.0), axis=0, keepdims=True)
        gate = jnp.where(hot, prob / pick_sum, 0.0)
        gate_bf = lax.reduce_precision(gate, 8, 7)
        earlier, before = running_count(hot.astype(F32))
        kept = hot & (earlier < capacity)
        pos = jnp.where(kept, earlier, -1.0).astype(jnp.int32)[:, None, :]
        cnt = jnp.minimum(before, capacity).astype(jnp.int32)

        y_acc = dx_acc = jnp.zeros((8, 128), F32)
        y_acc, dx_acc, a = token_side(True, cnt, pos, gate_bf[:, None, :], x_loc, dy_loc, *w_all, y_acc, dx_acc)
        a = a[:, 0]

        sent = jnp.where(kept, gate_bf, -1.0).reshape(n_dev, loc_exp, tok_count)
        got = lax.all_to_all(sent, "ep", 0, 0).reshape(n_dev, loc_exp, n_chunk, span)
        per_grp = n_chunk
        got = got.reshape(n_dev // per_grp, per_grp, loc_exp, n_chunk, span).transpose(3, 0, 2, 1, 4)
        got = got.reshape(-1, tok_count)
        own_hot = got >= 0.0
        own_pos, own_cnt = running_count(own_hot.astype(F32))
        own_pos = jnp.where(own_hot, own_pos, -1.0).astype(jnp.int32)[:, None, :]
        own_cnt = own_cnt.astype(jnp.int32)
        own_w = jnp.where(own_hot, got, 0.0)[:, None, :]
        accs = [jnp.zeros(a.shape, F32) for a in (wg_loc, wu_loc, wd_loc)]
        n_row = own_pos.shape[0] // n_chunk
        for c in range(n_chunk):
            part = slice(c * n_row, (c + 1) * n_row)
            accs = owner_side(c == 0, own_cnt[part], own_pos[part], own_w[part], *tok_all[c], wg_loc, wu_loc, wd_loc, accs)
        dw_gate, dw_up, dw_down = accs

        load_stats = jnp.concatenate([jnp.sum(hot.astype(F32), axis=1), jnp.sum(prob, axis=1)])
        load_stats = lax.psum(load_stats, "ep")
        load_frac = load_stats[:n_exp] / (n_total * top_k)
        mean_prob = load_stats[n_exp:] / n_total
        aux_loss = AUX_COEF * n_exp * jnp.sum(load_frac * mean_prob)

        d_pick = (a - jnp.sum(a * gate, axis=0, keepdims=True)) / pick_sum
        d_prob = jnp.where(hot, d_pick, 0.0) + (AUX_COEF * n_exp / n_total) * load_frac[:, None]
        d_logit = (prob * (d_prob - jnp.sum(prob * d_prob, axis=0, keepdims=True))).astype(BF16)
        dw_router = lax.dot_general(x_loc, d_logit, (((0,), (1,)), ((), ())), preferred_element_type=F32)
        dw_router = lax.psum(dw_router, "ep")
        dx_router = lax.dot_general(d_logit, w_router, (((0,), (1,)), ((), ())), preferred_element_type=F32)
        return y_acc.astype(BF16), aux_loss, (dx_acc + dx_router).astype(BF16), dw_router, dw_gate, dw_up, dw_down

    tok_spec = P("ep")
    return jax.shard_map(
        local_block,
        mesh=mesh,
        in_specs=(tok_spec, P(), tok_spec, tok_spec, tok_spec, tok_spec, tok_spec),
        out_specs=(tok_spec, P(), tok_spec, P(), tok_spec, tok_spec, tok_spec),
        check_vma=False,
    )
```

time: 3730 us -> 1100 us (0.29)
  local copies, waits for them, and re-layouts: 1330 us -> 26.4 us
  blocking collectives: 988 us -> 35.3 us
  Pallas kernels: 0 us -> 600 us
  waiting for transfers between devices: 854 us -> 391 us
  matrix products: 402 us -> 9.17 us
  other arithmetic: 100 us -> 14.1 us
    gather x13 -> x0, local copies, waits for them, and re-layouts: 1200 us -> none  [the longest x1 300 us: local_block(): dx_tok = jnp.take(back_dx, slot_ids, axis=0, mode='fill', fill_value=0)]
    all_to_all x3 -> x1, waiting for transfers between devices: 854 us -> 0.01 us  [local_block(): lax.all_to_all(sent, 'ep', 0, 0).reshape(n_dev, loc_exp, n_chunk, span)]
    pallas_call x0 -> x3, Pallas kernels: none -> 600 us  [the longest x1 334 us: token_side(): pl.pallas_call(functools.partial(token_kernel, first), grid_spec=pltpu.Pr...]
    psum x1, blocking collectives: 523 us -> 35.3 us  [local_block(): load_stats = lax.psum(load_stats, 'ep')]
    all_to_all x1 -> x0, blocking collectives: 465 us -> none  [local_block(): recv_do = lax.all_to_all(send_do, 'ep', 0, 1)]
    dot_general x14 -> x5, matrix products: 402 us -> 9.17 us  [the longest x1 3.54 us: local_block(): lax.dot_general(w_router, x_loc, (((0,), (1,)), ((), ())), preferred_elem...]
    all_gather x0 -> x7, waiting for transfers between devices: none -> 388 us  [local_block(): gather = lambda a: lax.all_gather(a, 'ep', axis=0, tiled=True)]
    scatter x1 -> x0, local copies, waits for them, and re-layouts: 60.4 us -> none  [route_slots(): empty_fill.at[slot_ids.reshape(-1)].set(pair_ids, mode='drop')]
  transfers between devices with their start and end apart: 4 -> 9, of which waited for: 2 -> 4; matrix products, arithmetic and copies ran while one was open for 25% -> 4% of each run, Pallas kernels for 0% -> 55%
where the time goes in v1:
time: 1100 us
  Pallas kernels  600 us (55%)
  waiting for transfers between devices  391 us (36%)
  blocking collectives  35.3 us (3%)
  local copies, waits for them, and re-layouts  26.4 us (2%)
  between operations  16.7 us (2%)
  other arithmetic  14.1 us (1%)
    all_gather x7, waiting for transfers between devices, local_block(): gather = lambda a: lax.all_gather(a, 'ep', axis=0, tiled=True)  388 us
    pallas_call x1, Pallas kernels, token_side(): pl.pallas_call(functools.partial(token_kernel, first), grid_spec=pltpu.Pr...  334 us
    pallas_call x2, Pallas kernels, owner_side(): pl.pallas_call(functools.partial(owner_kernel, first), grid_spec=pltpu.Pr...  266 us
    psum x1, blocking collectives, local_block(): load_stats = lax.psum(load_stats, 'ep')  35.3 us
  transfers between devices with their start and end apart: 9, of which 4 were waited for; matrix products, arithmetic and copies ran while one was open for 4% of the time, Pallas kernels for 55%

profile of v1, /device:TPU:0, one launch (start us, length us, event | category | flops | bytes accessed | tf_op | source)
XLA Modules:
  0.0 1095.9 jit_solution(10372897675533976456)
XLA Ops:
  7.2 0.7 all-gather.10.cloned.1.call-update
  7.9 0.7 all-gather.12.cloned.1.call-update
  8.7 0.7 all-gather.8.cloned.1.call-update
  9.4 4.6 fusion.29
  14.2 4.7 fusion.28
  18.9 0.5 all-gather.14.cloned.1.call-update
  19.5 0.7 all-gather.16.cloned.1.call-update
  20.2 0.2 slice_reduce_fusion.7
  20.6 0.3 convert_reduce_fusion
  20.9 0.1 copy.36
  21.0 0.1 select_reduce_fusion.2
  21.1 3.5 fusion.31
  24.7 0.4 fusion.27
  25.1 0.2 copy-done.25
  25.3 0.4 copy-done.27
  25.7 0.2 reduce-precision_bitcast_fusion
  26.0 0.3 copy-done.29
  26.3 1.0 copy.39.w_ref
  27.3 0.1 copy.38
  27.4 0.4 broadcast_compare_fusion
  27.7 0.3 reshape.424
  28.0 0.1 copy.48
  28.1 0.7 copy.50
  28.8 0.1 pad_maximum_fusion
  28.8 35.3 %psum.14 = f32[64]{0:T(128)S(1)} all-reduce(f32[64]{0:T(128)S(1)} %pad_maximum_fusion), channel_id=1, replica_groups=mesh['ep'=16] {'ep'}, use_global_device_ids=true, to_apply=%region_7.8 | all-reduce | flops 64 | bytes 512 | tf_op jit(solution)/shard_map/psum | solution.py:299
  64.2 1.1 slice_multiply_fusion
  65.9 0.6 minimum_convert_fusion.cnt_ref
  66.6 2.6 fusion.5.pos_ref
  69.2 76.6 %all-gather.10.cloned.1.call-done.wu_ref = bf16[32,1024,512]{2,1,0:T(8,128)(2,1)} async-done(((bf16[2,1024,512]{2,1,0:T(8,128)(2,1)}), bf16[32,1024,512]{2,1,0:T(8,128)(2,1)}) %all-gather.10.cloned.1.call-update) | async-done | bytes 33554448 | tf_op jit(solution)/shard_map/all_gather | solution.py:257
  145.8 133.5 %all-gather.12.cloned.1.call-done.wd_ref = bf16[32,512,1024]{2,1,0:T(8,128)(2,1)} async-done(((bf16[2,512,1024]{2,1,0:T(8,128)(2,1)}), bf16[32,512,1024]{2,1,0:T(8,128)(2,1)}) %all-gather.12.cloned.1.call-update) | async-done | bytes 33554448 | tf_op jit(solution)/shard_map/all_gather | solution.py:257
  279.4 133.6 %all-gather.8.cloned.1.call-done.wg_ref = bf16[32,1024,512]{2,1,0:T(8,128)(2,1)} async-done(((bf16[2,1024,512]{2,1,0:T(8,128)(2,1)}), bf16[32,1024,512]{2,1,0:T(8,128)(2,1)}) %all-gather.8.cloned.1.call-update) | async-done | bytes 33554448 | tf_op jit(solution)/shard_map/all_gather | solution.py:257
  412.9 0.6 broadcast_in_dim.78.y_in.dx_in
  413.5 333.8 %token_side.1 = (f32[2048,1024]{1,0:T(8,128)}, f32[2048,1024]{1,0:T(8,128)}, f32[32,1,2048]{2,1,0:T(1,128)}) custom-call(s32[32,5]{1,0:T(8,128)} %minimum_convert_fusion.cnt_ref, s32[32,1,2048]{2,1,0:T(1,128)} %fusion.5.pos_ref, f32[32,1,2048]{2,1,0:T(1,128)} %copy.39.w_ref, bf16[2048,1024]{1,0:T(8,128)(2,1)} %x_ref.1, bf16[2048,1024]{1,0:T(8,128)(2,1)} %dy_ref.1, ...), custom_call_target="tpu_custom_call" | custom-call | flops 257698037760 | bytes 104857600 | tf_op jit(solution)/shard_map/token_side/pallas_call | solution.py:144
  747.4 1.4 and_select_fusion.1
  748.8 0.8 reshape.425
  749.7 2.6 all-to-all-start
  752.4 6.3 convert_element_type.54
  758.8 0.3 multiply_reduce_fusion
  759.1 0.8 copy-done.3
  759.9 3.4 add_convert_fusion
  763.3 1.6 convolution_bitcast_fusion
  765.0 0.3 reshape_reshape.3
  765.3 0.3 compare_convert_fusion
  765.6 0.2 copy.40
  765.8 0.2 reshape.428
  766.0 0.1 reduce_sum.108
  766.1 0.1 copy.41
  766.2 0.1 select_reduce_fusion.1
  766.3 0.1 copy.43
  766.4 0.2 convolution_add_fusion
  766.6 0.1 copy.52
  766.7 0.1 copy.51
  766.9 0.8 copy.44.pos_ref
  767.7 0.8 copy.45.w_ref
  768.5 0.1 copy.49
  768.5 0.6 fusion.30
  769.1 0.8 copy.46.pos_ref
  769.9 0.7 slice.126.w_ref
  770.7 2.5 broadcast_1_ag_in_au_in.2.ag_in.au_in
  773.2 2.5 broadcast_in_dim.82.ad_in
  775.7 131.1 %owner_side.2 = (f32[2,1024,512]{2,1,0:T(8,128)}, f32[2,1024,512]{2,1,0:T(8,128)}, f32[2,512,1024]{2,1,0:T(8,128)}) custom-call(s32[16,5]{1,0:T(8,128)} %get-tuple-element.56.cnt_ref, s32[16,1,2048]{2,1,0:T(1,128)} %copy.44.pos_ref, f32[16,1,2048]{2,1,0:T(1,128)} %copy.45.w_ref, bf16[16384,1024]{1,0:T(8,128)(2,1)} %all-gather.18.cloned.1.call-done.x_ref, ...), custom_call_target="tpu_custom_call" | custom-call | flops 128849018880 | bytes 104857600 | tf_op jit(solution)/shard_map/owner_side/pallas_call | solution.py:215
  906.8 44.0 %all-gather.16.cloned.1.call-done.dy_ref = bf16[16384,1024]{1,0:T(8,128)(2,1)} async-done(((bf16[1024,1024]{1,0:T(8,128)(2,1)}), bf16[16384,1024]{1,0:T(8,128)(2,1)}) %all-gather.16.cloned.1.call-update) | async-done | bytes 33554448 | tf_op jit(solution)/shard_map/all_gather | solution.py:257
  950.8 135.4 %owner_side.3 = (f32[2,1024,512]{2,1,0:T(8,128)}, f32[2,1024,512]{2,1,0:T(8,128)}, f32[2,512,1024]{2,1,0:T(8,128)}) custom-call(s32[16,5]{1,0:T(8,128)} %get-tuple-element.57.cnt_ref, s32[16,1,2048]{2,1,0:T(1,128)} %copy.46.pos_ref, f32[16,1,2048]{2,1,0:T(1,128)} %slice.126.w_ref, ...), custom_call_target="tpu_custom_call", output_to_operand_aliasing={{0}: (8, {}), {1}: (9, {}), {2}: (10, {})} | custom-call | flops 128849018880 | bytes 104857600 | tf_op jit(solution)/shard_map/owner_side/pallas_call | solution.py:215
  1086.2 1.6 copy.66
  (99 shorter events, 0.8 us)
Async XLA Ops:
  7.2 138.7 %all-gather.10.cloned.1.call-start = ((), (), s32[]{:S(2)}) async-start(), calls=%async_computation.2 | async-start | bytes 35651584 | tf_op jit(solution)/shard_map/all_gather | solution.py:257
  7.9 271.5 %all-gather.12.cloned.1.call-start = ((), (), s32[]{:S(2)}) async-start(), calls=%async_computation.3 | async-start | bytes 35651584 | tf_op jit(solution)/shard_map/all_gather | solution.py:257
  8.6 404.3 %all-gather.8.cloned.1.call-start = ((), (), s32[]{:S(2)}) async-start(), calls=%async_computation.1 | async-start | bytes 35651584 | tf_op jit(solution)/shard_map/all_gather | solution.py:257
  9.4 761.3 %all-gather.18.cloned.1.call-start = ((), (), s32[]{:S(2)}) async-start(), calls=%async_computation.7 | async-start | bytes 35651584 | tf_op jit(solution)/shard_map/all_gather | solution.py:257
  14.1 756.6 %all-gather.20.cloned.1.call-start = ((), (), s32[]{:S(2)}) async-start(), calls=%async_computation.8 | async-start | bytes 35651584 | tf_op jit(solution)/shard_map/all_gather | solution.py:257
  18.8 1.4 copy-start.30
  18.8 2.3 copy-start.23
  18.8 887.9 %all-gather.14.cloned.1.call-start = ((), (), s32[]{:S(2)}) async-start(), calls=%async_computation.5 | async-start | bytes 35651584 | tf_op jit(solution)/shard_map/all_gather | solution.py:257
  19.4 931.3 %all-gather.16.cloned.1.call-start = ((), (), s32[]{:S(2)}) async-start(), calls=%async_computation.6 | async-start | bytes 35651584 | tf_op jit(solution)/shard_map/all_gather | solution.py:257
  20.4 46.2 %copy-start.5 = (s32[1,2048]{1,0:T(1,128)}, s32[1,2048]{1,0:T(1,128)S(1)}, u32[]{:S(2)}) copy-start(s32[1,2048]{1,0:T(1,128)S(1)} %get-tuple-element.48) | copy-start | bytes 24580
  20.4 46.2 %copy-start.7 = (s32[1,2048]{1,0:T(1,128)}, s32[1,2048]{1,0:T(1,128)S(1)}, u32[]{:S(2)}) copy-start(s32[1,2048]{1,0:T(1,128)S(1)} %get-tuple-element.49) | copy-start | bytes 24580
  20.4 46.2 %copy-start.9 = (s32[1,2048]{1,0:T(1,128)}, s32[1,2048]{1,0:T(1,128)S(1)}, u32[]{:S(2)}) copy-start(s32[1,2048]{1,0:T(1,128)S(1)} %get-tuple-element.50) | copy-start | bytes 24580
  20.4 46.2 %copy-start.11 = (s32[1,2048]{1,0:T(1,128)}, s32[1,2048]{1,0:T(1,128)S(1)}, u32[]{:S(2)}) copy-start(s32[1,2048]{1,0:T(1,128)S(1)} %get-tuple-element.51) | copy-start | bytes 24580
  20.4 46.1 %copy-start.13 = (s32[1,2048]{1,0:T(1,128)}, s32[1,2048]{1,0:T(1,128)S(1)}, u32[]{:S(2)}) copy-start(s32[1,2048]{1,0:T(1,128)S(1)} %get-tuple-element.52) | copy-start | bytes 24580
  20.4 46.1 %copy-start.15 = (s32[1,2048]{1,0:T(1,128)}, s32[1,2048]{1,0:T(1,128)S(1)}, u32[]{:S(2)}) copy-start(s32[1,2048]{1,0:T(1,128)S(1)} %get-tuple-element.53) | copy-start | bytes 24580
  20.4 46.1 %copy-start.17 = (s32[1,2048]{1,0:T(1,128)}, s32[1,2048]{1,0:T(1,128)S(1)}, u32[]{:S(2)}) copy-start(s32[1,2048]{1,0:T(1,128)S(1)} %get-tuple-element.54) | copy-start | bytes 24580
  20.5 46.1 %copy-start.19 = (s32[1,2048]{1,0:T(1,128)}, s32[1,2048]{1,0:T(1,128)S(1)}, u32[]{:S(2)}) copy-start(s32[1,2048]{1,0:T(1,128)S(1)} %get-tuple-element.55) | copy-start | bytes 24580
  21.0 6.8 copy-start.31
  24.6 1.1 copy-start.1
  24.6 1.3 copy-start.21
  24.7 0.6 copy-start.25
  25.1 0.6 copy-start.27
  25.7 0.6 copy-start.29
  413.5 333.8 %copy-start.6 = (s32[1,2048]{1,0:T(1,128)S(1)}, s32[1,2048]{1,0:T(1,128)}, u32[]{:S(2)}) copy-start(s32[1,2048]{1,0:T(1,128)} %copy-done.5) | copy-start | bytes 24580
  413.5 333.8 %copy-start.8 = (s32[1,2048]{1,0:T(1,128)S(1)}, s32[1,2048]{1,0:T(1,128)}, u32[]{:S(2)}) copy-start(s32[1,2048]{1,0:T(1,128)} %copy-done.7) | copy-start | bytes 24580
  413.5 333.8 %copy-start.10 = (s32[1,2048]{1,0:T(1,128)S(1)}, s32[1,2048]{1,0:T(1,128)}, u32[]{:S(2)}) copy-start(s32[1,2048]{1,0:T(1,128)} %copy-done.9) | copy-start | bytes 24580
  413.5 333.8 %copy-start.12 = (s32[1,2048]{1,0:T(1,128)S(1)}, s32[1,2048]{1,0:T(1,128)}, u32[]{:S(2)}) copy-start(s32[1,2048]{1,0:T(1,128)} %copy-done.11) | copy-start | bytes 24580
  413.5 333.9 %copy-start.14 = (s32[1,2048]{1,0:T(1,128)S(1)}, s32[1,2048]{1,0:T(1,128)}, u32[]{:S(2)}) copy-start(s32[1,2048]{1,0:T(1,128)} %copy-done.13) | copy-start | bytes 24580
  749.7 15.3 %all-to-all-start = ((f32[16,2,2048]{2,1,0:T(2,128)}), f32[16,2,2048]{2,1,0:T(2,128)S(1)}, u32[]{:S(2)}, u32[]{:S(2)}) async-start(f32[16,2,2048]{2,1,0:T(2,128)} %reshape.425), calls=%async_computation | async-start | bytes 524288 | tf_op jit(solution)/shard_map/all_to_all | solution.py:282
  752.2 333.9 %all-reduce.2.cloned.1.call-start = ((), (), s32[]{:S(2)}) async-start(), calls=%async_computation.4 | async-start | bytes 262144 | tf_op jit(solution)/shard_map/psum | solution.py:308
  752.3 6.5 copy-start.2
  752.3 6.5 copy-start.4
  752.3 6.4 copy-start.16
  752.3 6.4 copy-start.18
  752.3 6.4 copy-start.20
  752.3 6.4 copy-start.22
  752.3 6.4 copy-start.26
  752.4 6.4 copy-start.28
  752.4 6.4 copy-start.33
  752.4 7.5 copy-start.3
  752.4 7.5 copy-start.24
  759.9 3.4 copy-start
  763.3 2.9 copy-start.32
Sparse Core Ops, SparseCore 0:
  10.2 135.5 all-gather.9
  148.1 131.2 all-gather.11
  281.6 131.2 all-gather.7
  415.6 131.2 all-gather.17
  549.6 131.3 all-gather.19
  683.1 134.0 all-gather.13
  819.4 131.2 all-gather.15
  955.6 65.0 all-reduce.1

commit v2 on v1

v2 whole, which is shorter than its diff:
```python
import functools

import jax
import jax.numpy as jnp
from jax import lax
from jax.experimental import pallas as pl
from jax.experimental.pallas import tpu as pltpu
from jax.sharding import PartitionSpec as P


AUX_COEF = 0.001
SEG = 512
WIN = 192
TILE = 640
EAGER = True
F32, BF16 = jnp.float32, jnp.bfloat16


def mm(a, b, ca=1, cb=0):
    return lax.dot_general(a, b, (((ca,), (cb,)), ((), ())), preferred_element_type=F32)


def window(cnt_ref, row, b):
    start = (cnt_ref[row, b] // 16) * 16
    return pl.multiple_of(start, 16), jnp.maximum((cnt_ref[row, b + 1] - start + WIN - 1) // WIN, 1)


def hot_rows(pos_ref, b, start):
    pos = pos_ref[0, :, b * SEG:(b + 1) * SEG] - start
    return lax.broadcasted_iota(jnp.int32, (WIN, SEG), 0) == pos


def gather_rows(cnt_ref, row, pos_ref, w_ref, t_ref, xs, dys, ds, n_seg, n_rows):
    dim = xs.shape[1]
    end = 0
    for b in range(n_seg):
        first, n_win = window(cnt_ref, row, b)

        def step(c, _, b=b, first=first):
            start = pl.multiple_of(first + c * WIN, 16)
            hot = hot_rows(pos_ref, b, start)
            sel = hot.astype(F32).astype(BF16)
            tok = slice(b * SEG, (b + 1) * SEG)
            w_col = jnp.sum(jnp.where(hot, w_ref[0, :, tok], 0.0), axis=1, keepdims=True)
            both = mm(sel, t_ref[tok, :])
            x_new, dy_new = both[:, :dim], both[:, dim:]
            d_new = w_col * dy_new
            outs = [(xs, x_new), (ds, d_new)] + ([(dys, dy_new)] if dys is not None else [])
            for ref, new in outs:
                new = new.astype(BF16)
                ref[pl.ds(start + 16, WIN - 16), :] = new[16:]
                if b == 0:
                    ref[pl.ds(start, 16), :] = new[:16]
                else:
                    old = ref[pl.ds(start, 16), :].astype(F32)
                    keep = jnp.where(c == 0, 1.0, 0.0)
                    ref[pl.ds(start, 16), :] = (jnp.where(keep > 0, old, 0.0) + new[:16].astype(F32)).astype(BF16)
            return 0

        if EAGER:
            step(0, 0)
        lax.fori_loop(int(EAGER), n_win, step, 0)
        end = first + n_win * WIN

    def clear(i, _):
        at = pl.multiple_of(i * 16, 16)
        zero = jnp.zeros((16, dim), BF16)
        xs[pl.ds(at, 16), :] = zero
        ds[pl.ds(at, 16), :] = zero
        if dys is not None:
            dys[pl.ds(at, 16), :] = zero
        return 0

    lax.fori_loop(end // 16, n_rows // 16, clear, 0)


def slot_grads(x, d, w_ref, dim):
    pre = mm(x, w_ref[0, :dim, :])
    ff = pre.shape[1] // 2
    g, u = pre[:, :ff], pre[:, ff:]
    s = jax.nn.sigmoid(g)
    act = g * s
    h = (act * u).astype(BF16)
    dh = mm(d, w_ref[0, dim:, :], 1, 1).astype(BF16).astype(F32)
    dg = (dh * u * s * (1.0 + g * (1.0 - s))).astype(BF16)
    du = (dh * act).astype(BF16)
    return h, jnp.concatenate([dg, du], axis=1)


def token_kernel(first, counts, id_ref, src_ref, cnt_ref, pos_ref, w_ref, t_ref, *refs):
    n_src = len(counts)
    wt_refs = refs[:n_src]
    y_in, dx_in, _, _, y_out, dx_out, a_out, order, wt_buf, xs, dys, ds, os, dxs, y_acc, dx_acc, wt_sem, sems = refs[n_src:]
    i = pl.program_id(0)
    last = pl.num_programs(0) - 1
    row = id_ref[i]
    n_seg = t_ref.shape[0] // SEG
    dim = xs.shape[1]

    def fetch(step):
        lo = 0
        for ref, n in zip(wt_refs, counts):
            @pl.when((step >= lo) & (step < lo + n))
            def _(ref=ref):
                pltpu.make_async_copy(ref.at[src_ref[step]], wt_buf.at[step % 2], wt_sem.at[step % 2]).start()

            lo += n

    def loads():
        return [pltpu.make_async_copy(y_in, y_acc, sems.at[0, 0]), pltpu.make_async_copy(dx_in, dx_acc, sems.at[1, 0])]

    @pl.when(i == 0)
    def _():
        fetch(i)
        if first:
            y_acc[...] = jnp.zeros_like(y_acc)
            dx_acc[...] = jnp.zeros_like(dx_acc)
        else:
            for copy in loads():
                copy.start()
        os[TILE:, :] = jnp.zeros((WIN, dim), BF16)
        dxs[TILE:, :] = jnp.zeros((WIN, dim), BF16)
        order[...] = jnp.zeros_like(order)

    @pl.when(i < last)
    def _():
        fetch(i + 1)

    gather_rows(cnt_ref, row, pos_ref, w_ref, t_ref, xs, dys, ds, n_seg, TILE)
    pltpu.make_async_copy(wt_refs[0].at[0], wt_buf.at[i % 2], wt_sem.at[i % 2]).wait()
    wt = wt_buf.at[pl.ds(i % 2, 1)]
    h, dgu = slot_grads(xs[:TILE, :], ds[:TILE, :], wt, dim)
    os[:TILE, :] = mm(h, wt[0, dim:, :]).astype(BF16)
    dxs[:TILE, :] = mm(dgu, wt[0, :dim, :], 1, 1).astype(BF16)
    if not first:
        @pl.when(i == 0)
        def _():
            for copy in loads():
                copy.wait()

    stores = []
    for b in range(n_seg):
        start0, n_win = window(cnt_ref, row, b)
        tok = slice(b * SEG, (b + 1) * SEG)

        def step(c, a_row, b=b, start0=start0, tok=tok):
            start = pl.multiple_of(start0 + c * WIN, 16)
            hot = hot_rows(pos_ref, b, start)
            sel = hot.astype(F32)
            sel_w = jnp.where(hot, w_ref[0, :, tok], 0.0).astype(BF16)
            o_win = os[pl.ds(start, WIN), :]
            y_acc[tok, :] += mm(sel_w, o_win, 0, 0)
            dx_acc[tok, :] += mm(sel.astype(BF16), dxs[pl.ds(start, WIN), :], 0, 0)
            a_col = jnp.sum(o_win.astype(F32) * dys[pl.ds(start, WIN), :].astype(F32), axis=1, keepdims=True)
            return a_row + jnp.sum(jnp.where(hot, a_col, 0.0), axis=0, keepdims=True)

        a_row = jnp.zeros((1, SEG), F32)
        if EAGER:
            a_row = step(0, a_row)
        a_out[0, :, tok] = lax.fori_loop(int(EAGER), n_win, step, a_row)
        part = pl.ds(b * SEG, SEG)
        done = [pltpu.make_async_copy(y_acc.at[part], y_out.at[part], sems.at[0, b]),
                pltpu.make_async_copy(dx_acc.at[part], dx_out.at[part], sems.at[1, b])]
        stores += done

        @pl.when(i == last)
        def _(done=done):
            for copy in done:
                copy.start()

    @pl.when(i == last)
    def _():
        for copy in stores:
            copy.wait()


def token_side(first, ids, srcs, counts, cnt, pos, w, t, wts, y_in, dx_in, a_in, after):
    n_exp, _, tok_count = pos.shape
    _, w_rows, dim = wts[0].shape
    n_here, n_src = sum(counts), len(counts)
    row_spec = pl.BlockSpec((1, 1, tok_count), lambda i, ids, *_: (ids[i], 0, 0))
    any_spec = pl.BlockSpec(memory_space=pl.ANY)
    acc_shape = jax.ShapeDtypeStruct((tok_count, dim), F32)
    at = 6 + n_src
    return pl.pallas_call(
        functools.partial(token_kernel, first, counts),
        grid_spec=pltpu.PrefetchScalarGridSpec(
            num_scalar_prefetch=3,
            grid=(n_here,),
            in_specs=[row_spec, row_spec, pl.BlockSpec(t.shape, lambda i, *_: (0, 0), pipeline_mode=pl.Buffered(1))]
            + [any_spec] * (n_src + 4),
            out_specs=[any_spec, any_spec, row_spec, pl.BlockSpec((8, 128), lambda i, *_: (0, 0))],
            scratch_shapes=[pltpu.VMEM((2, w_rows, dim), BF16)] + [pltpu.VMEM((TILE + WIN, dim), BF16)] * 5
            + [pltpu.VMEM((tok_count, dim), F32)] * 2
            + [pltpu.SemaphoreType.DMA((2,)), pltpu.SemaphoreType.DMA((2, tok_count // SEG))],
        ),
        out_shape=[acc_shape, acc_shape, jax.ShapeDtypeStruct((n_exp, 1, tok_count), F32), jax.ShapeDtypeStruct((8, 128), F32)],
        input_output_aliases={at + 2: 2} if first else {at: 0, at + 1: 1, at + 2: 2},
        compiler_params=pltpu.CompilerParams(dimension_semantics=("arbitrary",), vmem_limit_bytes=67000000),
        cost_estimate=pl.CostEstimate(flops=n_here * 2 * 4 * 640 * w_rows * dim, bytes_accessed=50 << 20, transcendentals=0),
        name="token_side",
    )(ids, srcs, cnt, pos, w, t, *wts, y_in, dx_in, a_in, after)


def owner_kernel(first, cnt_ref, pos_ref, w_ref, t_ref, wt_ref, acc_in, after, acc_out, order, xs, ds, acc, sem):
    g, e = pl.program_id(0), pl.program_id(1)
    n_grp, n_exp = pl.num_programs(0), pl.num_programs(1)
    n_seg = t_ref.shape[0] // SEG
    dim = xs.shape[1]
    row = g * n_exp + e

    @pl.when((g == 0) & (e == 0))
    def _():
        if first:
            acc[...] = jnp.zeros_like(acc)
        else:
            for k in range(acc.shape[0]):
                pltpu.make_async_copy(acc_in.at[k], acc.at[k], sem.at[k]).start()
        order[...] = jnp.zeros_like(order)

    n_tile = (cnt_ref[row, n_seg] + TILE - 1) // TILE
    gather_rows(cnt_ref, row, pos_ref, w_ref, t_ref, xs, None, ds, n_seg, n_tile * TILE)
    if not first:
        @pl.when(g == 0)
        def _():
            pltpu.make_async_copy(acc_in.at[e], acc.at[e], sem.at[e]).wait()

    def tile(t, _):
        at = pl.multiple_of(t * TILE, 16)
        x, d = xs[pl.ds(at, TILE), :], ds[pl.ds(at, TILE), :]
        h, dgu = slot_grads(x, d, wt_ref, dim)
        acc[e, dim:, :] += mm(h, d, 0, 0)
        acc[e, :dim, :] += mm(x, dgu, 0, 0)
        return 0

    lax.fori_loop(0, n_tile, tile, 0)

    @pl.when(g == n_grp - 1)
    def _():
        pltpu.make_async_copy(acc.at[e], acc_out.at[e], sem.at[e]).start()

    @pl.when((g == n_grp - 1) & (e == n_exp - 1))
    def _():
        for k in range(acc.shape[0]):
            pltpu.make_async_copy(acc.at[k], acc_out.at[k], sem.at[k]).wait()


def owner_side(first, cnt, pos, w, t, wt, acc, after):
    n_exp, w_rows, dim = wt.shape
    grp = pos.shape[2]
    n_grp = t.shape[0] // grp
    per_row = pl.BlockSpec((1, 1, grp), lambda g, e, c: (g * n_exp + e, 0, 0))
    any_spec = pl.BlockSpec(memory_space=pl.ANY)
    rows = -(-grp // TILE) * TILE + WIN
    return pl.pallas_call(
        functools.partial(owner_kernel, first),
        grid_spec=pltpu.PrefetchScalarGridSpec(
            num_scalar_prefetch=1,
            grid=(n_grp, n_exp),
            in_specs=[per_row, per_row, pl.BlockSpec((grp, t.shape[1]), lambda g, e, c: (g, 0)),
                      pl.BlockSpec((1, w_rows, dim), lambda g, e, c: (e, 0, 0)), any_spec, any_spec],
            out_specs=[any_spec, pl.BlockSpec((8, 128), lambda g, e, c: (0, 0))],
            scratch_shapes=[pltpu.VMEM((rows, dim), BF16)] * 2
            + [pltpu.VMEM((n_exp, w_rows, dim), F32), pltpu.SemaphoreType.DMA((n_exp,))],
        ),
        out_shape=[jax.ShapeDtypeStruct(wt.shape, F32), jax.ShapeDtypeStruct((8, 128), F32)],
        input_output_aliases={} if first else {5: 0},
        compiler_params=pltpu.CompilerParams(dimension_semantics=("arbitrary", "arbitrary"), vmem_limit_bytes=67000000),
        cost_estimate=pl.CostEstimate(flops=n_grp * n_exp * 2 * 4 * 640 * w_rows * dim, bytes_accessed=50 << 20, transcendentals=0),
        name="owner_side",
    )(cnt, pos, w, t, wt, acc, after)


def running_count(hot):
    rows, width = hot.shape
    blocks = hot.reshape(rows, width // 256, 256)
    upper = (jnp.arange(256)[:, None] < jnp.arange(256)[None, :]).astype(BF16)
    inside = jnp.einsum("rbi,ij->rbj", blocks.astype(BF16), upper, preferred_element_type=F32)
    total = jnp.sum(blocks, axis=2)
    n_blk = width // 256
    before = jnp.sum(jnp.where(jnp.arange(n_blk)[:, None] < jnp.arange(n_blk + 1)[None, :], total[:, :, None], 0.0), axis=1)
    return (inside + before[:, :-1, None]).reshape(rows, width), before[:, ::SEG // 256]


def solution(mesh):
    n_dev = mesh.shape["ep"]
    planes = [[d for d in range(n_dev) if d // 2 % 2 == x] for x in range(2)]
    across = [(d, d ^ 2) for d in range(n_dev)]
    beside = [(d, d ^ 1) for d in range(n_dev)]
    n_plane = n_dev // 2

    def local_block(x_loc, w_router, wg_loc, wu_loc, wd_loc, idx_loc, dy_loc):
        tok_count, dim = x_loc.shape
        top_k = idx_loc.shape[1]
        n_exp = w_router.shape[1]
        loc_exp = wg_loc.shape[0]
        ff = wg_loc.shape[2]
        capacity = (5 * tok_count * top_k + 4 * n_exp - 1) // (4 * n_exp)
        n_total = tok_count * n_dev
        n_half = 2
        span = tok_count // n_half
        me = lax.axis_index("ep")
        my_chip, my_x, my_core = me // 4, me // 2 % 2, me % 2
        share = lambda a: lax.all_to_all(jnp.broadcast_to(a, (n_dev,) + a.shape), "ep", 0, 0)
        plane_gather = lambda a: lax.all_gather(a, "ep", axis=0, tiled=True, axis_index_groups=planes)

        t_loc = jnp.concatenate([x_loc, dy_loc], axis=1)
        wt_loc = jnp.concatenate([jnp.concatenate([wg_loc, wu_loc], axis=2), wd_loc], axis=1)
        wt_nbr = lax.ppermute(wt_loc, "ep", across)
        wt_par = lax.ppermute(wt_loc, "ep", beside)
        nbr_par = lax.ppermute(wt_nbr[:1], "ep", beside)
        odd_plane = plane_gather(wt_loc[1:])
        t_all = [plane_gather(t_loc[c * span:(c + 1) * span]) for c in range(n_half)]
        even_plane = plane_gather(wt_loc[:1])
        even_nbr = plane_gather(wt_nbr[:1])
        mine = lax.dynamic_slice_in_dim(odd_plane, my_core * (n_plane // 2), n_plane // 2, 0)
        odd_nbr = lax.ppermute(mine, "ep", across)
        odd_nbr_par = lax.ppermute(odd_nbr, "ep", beside)

        idx_t = idx_loc.T
        exp_id = jnp.arange(n_exp, dtype=jnp.int32)[:, None]
        hot = exp_id == idx_t[0:1]
        for k in range(1, top_k):
            hot = hot | (exp_id == idx_t[k:k + 1])
        logits = lax.dot_general(w_router, x_loc, (((0,), (1,)), ((), ())), preferred_element_type=F32)
        prob = jax.nn.softmax(logits, axis=0)
        pick_sum = jnp.sum(jnp.where(hot, prob, 0.0), axis=0, keepdims=True)
        gate = jnp.where(hot, prob / pick_sum, 0.0)
        gate_bf = lax.reduce_precision(gate, 8, 7)
        earlier, before = running_count(hot.astype(F32))
        kept = hot & (earlier < capacity)
        pos = jnp.where(kept, earlier, -1.0).astype(jnp.int32)[:, None, :]
        cnt = jnp.minimum(before, capacity).astype(jnp.int32)

        sent = jnp.where(kept, gate_bf, -1.0).reshape(n_plane // 2, 2, 2, loc_exp, tok_count)
        sent = sent.transpose(0, 2, 1, 3, 4).reshape(n_plane, 2 * loc_exp, tok_count)
        got = lax.all_to_all(sent, "ep", 0, 0, axis_index_groups=planes)
        got = got.reshape(n_plane // n_half, n_half, 2, loc_exp, n_half, span).transpose(2, 4, 0, 3, 1, 5)
        got = jnp.where(my_x == 0, got[::-1], got).reshape(-1, tok_count)
        own_hot = got >= 0.0
        own_pos, own_cnt = running_count(own_hot.astype(F32))
        own_pos = jnp.where(own_hot, own_pos, -1.0).astype(jnp.int32)[:, None, :]
        own_cnt = own_cnt.astype(jnp.int32)
        own_w = jnp.where(own_hot, got, 0.0)[:, None, :]
        n_row = own_pos.shape[0] // (2 * n_half)

        zero = jnp.zeros((8, 128), F32)
        state = [zero, zero, jnp.zeros((n_exp, 1, tok_count), F32), zero]
        rest = jnp.arange(2 * n_plane // 2 - 2, dtype=jnp.int32)
        rest = (my_chip ^ (rest // 2 + 1)) * 2 + rest % 2
        expert = lambda place, x, j: (place // 2 * 4 + 2 * x + place % 2) * loc_exp + j
        quarter = jnp.arange(n_plane // 2, dtype=jnp.int32)
        pair = jnp.arange(loc_exp, dtype=jnp.int32)
        row_w = gate_bf[:, None, :]

        def run_token(parts, state):
            ids = jnp.concatenate([p[1] for p in parts])
            srcs = jnp.concatenate([p[2] for p in parts])
            counts = tuple(p[1].shape[0] for p in parts)
            first = state[0].shape == zero.shape
            return token_side(first, ids, srcs, counts, cnt, pos, row_w, t_loc, [p[0] for p in parts], *state)

        one = jnp.zeros((1,), jnp.int32)
        state = run_token([(wt_loc, me * loc_exp + pair, pair), (wt_par, (me ^ 1) * loc_exp + pair, pair)], state)
        state = run_token([(odd_plane, expert(rest, my_x, 1), rest), (wt_nbr, (me ^ 2) * loc_exp + one, one),
                           (nbr_par, (me ^ 3) * loc_exp + one, one)], state)
        sums = [zero, zero]
        order = state[3]
        for c in range(n_half):
            for p, wt in enumerate((wt_nbr, wt_loc)):
                part = slice((p * n_half + c) * n_row, (p * n_half + c + 1) * n_row)
                sums[p], order = owner_side(c == 0, own_cnt[part], own_pos[part], own_w[part], t_all[c], wt, sums[p], order)
        from_nbr = lax.ppermute(sums[0], "ep", across)
        half = n_plane // 2
        state = run_token([(odd_nbr, expert(my_core * half + quarter, 1 - my_x, 1), quarter),
                           (odd_nbr_par, expert((1 - my_core) * half + quarter, 1 - my_x, 1), quarter),
                           (even_plane, expert(rest, my_x, 0), rest)], [*state[:3], order])
        y_acc, dx_acc, a, _ = run_token([(even_nbr, expert(rest, 1 - my_x, 0), rest)], state)
        a = a[:, 0]

        load_stats = jnp.concatenate([jnp.sum(hot.astype(F32), axis=1), jnp.sum(prob, axis=1)])
        load_stats = jnp.sum(share(load_stats), axis=0)
        load_frac = load_stats[:n_exp] / (n_total * top_k)
        mean_prob = load_stats[n_exp:] / n_total
        aux_loss = AUX_COEF * n_exp * jnp.sum(load_frac * mean_prob)

        d_pick = (a - jnp.sum(a * gate, axis=0, keepdims=True)) / pick_sum
        d_prob = jnp.where(hot, d_pick, 0.0) + (AUX_COEF * n_exp / n_total) * load_frac[:, None]
        d_logit = (prob * (d_prob - jnp.sum(prob * d_prob, axis=0, keepdims=True))).astype(BF16)
        dw_router = lax.dot_general(d_logit, x_loc, (((1,), (0,)), ((), ())), preferred_element_type=F32)
        parts = lax.all_to_all(dw_router.reshape(n_exp, n_dev, dim // n_dev).transpose(1, 0, 2), "ep", 0, 0)
        dw_router = share(jnp.sum(parts, axis=0).T).reshape(dim, n_exp)
        dx_router = lax.dot_general(d_logit, w_router, (((0,), (1,)), ((), ())), preferred_element_type=F32)
        dw = sums[1] + from_nbr
        return (y_acc.astype(BF16), aux_loss, (dx_acc + dx_router).astype(BF16), dw_router,
                dw[:, :dim, :ff], dw[:, :dim, ff:], dw[:, dim:])

    tok_spec = P("ep")
    return jax.shard_map(
        local_block,
        mesh=mesh,
        in_specs=(tok_spec, P(), tok_spec, tok_spec, tok_spec, tok_spec, tok_spec),
        out_specs=(tok_spec, P(), tok_spec, P(), tok_spec, tok_spec, tok_spec),
        check_vma=False,
    )
```

time: 1100 us -> 1020 us (0.927)
  waiting for transfers between devices: 391 us -> 218 us
  Pallas kernels: 600 us -> 642 us
  blocking collectives: 35.3 us -> 0 us
  local copies, waits for them, and re-layouts: 26.4 us -> 56 us
  other arithmetic: 14.1 us -> 42.7 us
  starting transfers between devices: 2.87 us -> 19.3 us
    all_gather x7 -> x5, waiting for transfers between devices: 388 us -> 95.5 us  [local_block(): lax.all_gather(a, 'ep', axis=0, tiled=True, axis_index_groups=planes)]
    ppermute x0 -> x6, waiting for transfers between devices: none -> 100 us  [the longest x1 100 us: local_block(): odd_nbr = lax.ppermute(mine, 'ep', across)]
    psum x1 -> x0, blocking collectives: 35.3 us -> none  [local_block(): load_stats = lax.psum(load_stats, 'ep')]
    pallas_call x1 -> x4, Pallas kernels: 334 us -> 364 us  [token_side(): pl.pallas_call(functools.partial(token_kernel, first, counts), grid_spec=...]
    all_to_all x1 -> x4, waiting for transfers between devices: 0.01 us -> 21.3 us  [the longest x2 14 us: local_block(): lax.all_to_all(jnp.broadcast_to(a, (n_dev,) + a.shape), 'ep', 0, 0)]
    pallas_call x2 -> x4, Pallas kernels: 266 us -> 278 us  [owner_side(): pl.pallas_call(functools.partial(owner_kernel, first), grid_spec=pltpu.Pr...]
    dynamic_slice x0 -> x1, local copies, waits for them, and re-layouts: none -> 11.1 us  [local_block(): lax.dynamic_slice_in_dim(odd_plane, my_core * (n_plane // 2), n_plane //...]
  transfers between devices with their start and end apart: 9 -> 15, of which waited for: 4 -> 5; matrix products, arithmetic and copies ran while one was open for 4% -> 8% of each run, Pallas kernels for 55% -> 64%
where the time goes in v2:
time: 1020 us; the launch traced here: 1010 us
  Pallas kernels  642 us (63%)
  waiting for transfers between devices  218 us (21%)
  local copies, waits for them, and re-layouts  56 us (5%)
  other arithmetic  42.7 us (4%)
  starting transfers between devices  19.3 us (2%)
  between operations  17 us (2%)
  matrix products  12.2 us (1%)
    pallas_call x4, Pallas kernels, token_side(): pl.pallas_call(functools.partial(token_kernel, first, counts), grid_spec=...  364 us
    pallas_call x4, Pallas kernels, owner_side(): pl.pallas_call(functools.partial(owner_kernel, first), grid_spec=pltpu.Pr...  278 us
    ppermute x1, waiting for transfers between devices, local_block(): odd_nbr = lax.ppermute(mine, 'ep', across)  100 us
    all_gather x5, waiting for transfers between devices, local_block(): lax.all_gather(a, 'ep', axis=0, tiled=True, axis_index_groups=planes)  95.5 us
  transfers between devices with their start and end apart: 15, of which 5 were waited for; matrix products, arithmetic and copies ran while one was open for 8% of the time, Pallas kernels for 64%

profile of v2, /device:TPU:0, one launch (start us, length us, event | category | flops | bytes accessed | tf_op | source)
XLA Modules:
  0.0 1007.3 jit_solution(7553612737733533572)
XLA Ops:
  7.2 3.6 pad_maximum_fusion.refs_0_.wt_ref
  10.9 2.6 copy-done
  13.5 3.4 fusion.41
  17.0 2.8 constant_dynamic-update-slice_fusion.1
  19.8 0.6 copy-done.5
  20.4 0.6 constant_dynamic-update-slice_fusion.t_ref
  21.1 3.8 fusion.40
  24.8 3.5 copy-done.1
  28.4 0.7 all-gather.12.cloned.1.call-update
  29.7 0.9 collective-permute-start.4
  30.6 3.0 collective-permute-start
  33.6 3.5 fusion.43
  38.0 0.6 broadcast_in_dim.89
  38.6 2.8 all-to-all-start.1
  45.3 0.6 minimum_convert_fusion.cnt_ref
  45.9 95.5 %all-gather.8.cloned.1.call-done.refs_0_ = bf16[8,1536,1024]{2,1,0:T(8,128)(2,1)} async-done(((bf16[1,1536,1024]{2,1,0:T(8,128)(2,1)}), bf16[8,1536,1024]{2,1,0:T(8,128)(2,1)}) %all-gather.8.cloned.1.call-update) | async-done | bytes 25165840 | tf_op jit(solution)/shard_map/all_gather | solution.py:305
  141.3 11.1 %constant_dynamic-slice_fusion = bf16[4,1536,1024]{2,1,0:T(8,128)(2,1)} fusion(bf16[8,1536,1024]{2,1,0:T(8,128)(2,1)} %all-gather.8.cloned.1.call-done.refs_0_, s32[]{:T(128)S(6)} %select_n.123), kind=kLoop, calls=%fused_computation.122 | loop fusion | bytes 25165828 | tf_op jit(solution)/shard_map/dynamic_slice | solution.py:316
  152.4 1.5 collective-permute-start.1
  154.0 2.6 fusion.5.pos_ref
  158.0 0.9 copy.130
  158.9 14.0 %all-to-all-done.1 = f32[16,1,64]{2,1,0:T(1,128)S(1)} async-done(((f32[16,1,64]{2,1,0:T(1,128)}), f32[16,1,64]{2,1,0:T(1,128)S(1)}, u32[]{:S(2)}, u32[]{:S(2)}) %all-to-all-start.1) | async-done | bytes 4128 | tf_op jit(solution)/shard_map/all_to_all | solution.py:304
  172.9 3.4 all-to-all-start
  176.5 0.7 pad_add_fusion.id_ref
  177.7 0.9 broadcast_in_dim.83.w_ref
  178.7 1.1 slice_multiply_fusion
  180.4 5.9 all-to-all-done
  188.4 3.9 slice.202
  192.3 0.7 copy.138.pos_ref
  193.0 0.7 copy.139.w_ref
  193.8 0.7 copy.140.pos_ref
  194.5 0.7 copy.141.w_ref
  195.2 0.7 copy.142.pos_ref
  195.9 0.7 copy.143.w_ref
  196.6 0.7 copy.144.pos_ref
  197.2 0.7 copy.145.w_ref
  198.0 0.6 fusion.42
  199.2 0.8 broadcast_in_dim.85.clone.refs_4_
  200.0 49.9 %token_side.4 = (f32[2048,1024]{1,0:T(8,128)}, f32[2048,1024]{1,0:T(8,128)}, f32[32,1,2048]{2,1,0:T(1,128)}, f32[8,128]{1,0:T(8,128)}) custom-call(s32[4]{0:T(128)} %pad_add_fusion.3.id_ref, s32[4]{0:T(128)} %pad_add_fusion.4.src_ref, s32[32,5]{1,0:T(8,128)} %minimum_convert_fusion.cnt_ref, ...), custom_call_target="tpu_custom_call", output_to_operand_aliasing={{2}: (10, {})} | custom-call | flops 32212254720 | bytes 52428800 | tf_op jit(solution)/shard_map/token_side/pallas_call | solution.py:185
  249.9 89.8 %token_side.5 = (f32[2048,1024]{1,0:T(8,128)}, f32[2048,1024]{1,0:T(8,128)}, f32[32,1,2048]{2,1,0:T(1,128)}, f32[8,128]{1,0:T(8,128)}) custom-call(s32[8]{0:T(128)} %pad_add_fusion.2.id_ref, s32[8]{0:T(128)} %concatenate.36.src_ref, s32[32,5]{1,0:T(8,128)} %minimum_convert_fusion.cnt_ref, ...), custom_call_target="tpu_custom_call", output_to_operand_aliasing={{0}: (9, {}), {1}: (10, {}), {2}: (11, {})} | custom-call | flops 64424509440 | bytes 52428800 | tf_op jit(solution)/shard_map/token_side/pallas_call | solution.py:185
  339.7 100.1 %collective-permute-done.1.refs_0_ = bf16[4,1536,1024]{2,1,0:T(8,128)(2,1)} collective-permute-done((bf16[4,1536,1024]{2,1,0:T(8,128)(2,1)}, bf16[4,1536,1024]{2,1,0:T(8,128)(2,1)}, u32[]{:S(2)}, u32[]{:S(2)}) %collective-permute-start.1) | collective-permute-done | bytes 12582944 | tf_op jit(solution)/shard_map/ppermute | solution.py:317
  439.8 69.3 %owner_side.4 = (f32[2,1536,1024]{2,1,0:T(8,128)}, f32[8,128]{1,0:T(8,128)}) custom-call(s32[8,5]{1,0:T(8,128)} %get-tuple-element.95.cnt_ref, s32[8,1,2048]{2,1,0:T(1,128)} %copy.138.pos_ref, f32[8,1,2048]{2,1,0:T(1,128)} %copy.139.w_ref, bf16[8192,2048]{1,0:T(8,128)(2,1)} %all-gather.14.cloned.1.call-done.t_ref, ...), custom_call_target="tpu_custom_call" | custom-call | flops 64424509440 | bytes 52428800 | tf_op jit(solution)/shard_map/owner_side/pallas_call | solution.py:255
  509.2 69.6 %owner_side.5 = (f32[2,1536,1024]{2,1,0:T(8,128)}, f32[8,128]{1,0:T(8,128)}) custom-call(s32[8,5]{1,0:T(8,128)} %get-tuple-element.96.cnt_ref, s32[8,1,2048]{2,1,0:T(1,128)} %copy.140.pos_ref, f32[8,1,2048]{2,1,0:T(1,128)} %copy.141.w_ref, bf16[8192,2048]{1,0:T(8,128)(2,1)} %all-gather.14.cloned.1.call-done.t_ref, bf16[2,1536,1024]{2,1,0:T(8,128)(2,1)} %copy-done, ...), custom_call_target="tpu_custom_call" | custom-call | flops 64424509440 | bytes 52428800 | tf_op jit(solution)/shard_map/owner_side/pallas_call | solution.py:255
  578.8 69.7 %owner_side.6 = (f32[2,1536,1024]{2,1,0:T(8,128)}, f32[8,128]{1,0:T(8,128)}) custom-call(s32[8,5]{1,0:T(8,128)} %get-tuple-element.94.cnt_ref, s32[8,1,2048]{2,1,0:T(1,128)} %copy.142.pos_ref, f32[8,1,2048]{2,1,0:T(1,128)} %copy.143.w_ref, bf16[8192,2048]{1,0:T(8,128)(2,1)} %all-gather.12.cloned.1.call-done.t_ref, ...), custom_call_target="tpu_custom_call", output_to_operand_aliasing={{0}: (5, {})} | custom-call | flops 64424509440 | bytes 52428800 | tf_op jit(solution)/shard_map/owner_side/pallas_call | solution.py:255
  648.5 2.0 collective-permute-start.5
  650.5 69.5 %owner_side.7 = (f32[2,1536,1024]{2,1,0:T(8,128)}, f32[8,128]{1,0:T(8,128)}) custom-call(s32[8,5]{1,0:T(8,128)} %get-tuple-element.97.cnt_ref, s32[8,1,2048]{2,1,0:T(1,128)} %copy.144.pos_ref, f32[8,1,2048]{2,1,0:T(1,128)} %copy.145.w_ref, bf16[8192,2048]{1,0:T(8,128)(2,1)} %all-gather.12.cloned.1.call-done.t_ref, ...), custom_call_target="tpu_custom_call", output_to_operand_aliasing={{0}: (5, {})} | custom-call | flops 64424509440 | bytes 52428800 | tf_op jit(solution)/shard_map/owner_side/pallas_call | solution.py:255
  720.0 150.2 %token_side.6 = (f32[2048,1024]{1,0:T(8,128)}, f32[2048,1024]{1,0:T(8,128)}, f32[32,1,2048]{2,1,0:T(1,128)}, f32[8,128]{1,0:T(8,128)}) custom-call(s32[14]{0:T(128)} %pad_add_fusion.id_ref, s32[14]{0:T(128)} %pad_add_fusion.1.src_ref, s32[32,5]{1,0:T(8,128)} %minimum_convert_fusion.cnt_ref, ...), custom_call_target="tpu_custom_call", output_to_operand_aliasing={{0}: (9, {}), {1}: (10, {}), {2}: (11, {})} | custom-call | flops 112742891520 | bytes 52428800 | tf_op jit(solution)/shard_map/token_side/pallas_call | solution.py:185
  870.3 73.8 %token_side.7 = (f32[2048,1024]{1,0:T(8,128)}, f32[2048,1024]{1,0:T(8,128)}, f32[32,1,2048]{2,1,0:T(1,128)}, f32[8,128]{1,0:T(8,128)}) custom-call(s32[6]{0:T(128)} %add_multiply_fusion.1.id_ref, s32[6]{0:T(128)} %copy-done.33, s32[32,5]{1,0:T(8,128)} %minimum_convert_fusion.cnt_ref, ...), custom_call_target="tpu_custom_call", output_to_operand_aliasing={{0}: (7, {}), {1}: (8, {}), {2}: (9, {})} | custom-call | flops 48318382080 | bytes 52428800 | tf_op jit(solution)/shard_map/token_side/pallas_call | solution.py:185
  944.3 1.5 fusion.1
  945.7 1.4 multiply_reduce_fusion
  947.1 3.4 fusion.36
  950.7 0.8 reshape.497
  951.5 3.0 all-to-all-start.2
  954.6 4.8 fusion.37
  959.4 1.4 all-to-all-done.2
  961.3 0.9 reduce.33
  962.4 0.8 reshape.499
  963.3 2.4 all-to-all-start.3
  965.7 9.3 add_convert_fusion
  975.0 6.1 convert_element_type.59
  981.0 1.0 reduce.34
  982.3 0.8 reshape.451
  983.0 9.4 add.194
  992.5 4.4 fusion.39
  996.9 2.3 slice.222
  (156 shorter events, 11.3 us)
Async XLA Ops:
  7.2 134.2 %all-gather.8.cloned.1.call-start = ((), (), s32[]{:S(2)}) async-start(), calls=%async_computation.5 | async-start | bytes 28311552 | tf_op jit(solution)/shard_map/all_gather | solution.py:305
  10.9 2.6 copy-start
  16.9 422.9 %all-gather.14.cloned.1.call-start = ((), (), s32[]{:S(2)}) async-start(), calls=%async_computation.8 | async-start | bytes 37748736 | tf_op jit(solution)/shard_map/all_gather | solution.py:305
  16.9 3.5 copy-start.5
  21.0 7.3 copy-start.1
  28.4 5.2 copy-start.28
  28.4 8.9 copy-start.31
  28.4 550.4 %all-gather.12.cloned.1.call-start = ((), (), s32[]{:S(2)}) async-start(), calls=%async_computation.7 | async-start | bytes 37748736 | tf_op jit(solution)/shard_map/all_gather | solution.py:305
  29.1 690.9 %all-gather.10.cloned.1.call-start = ((), (), s32[]{:S(2)}) async-start(), calls=%async_computation.6 | async-start | bytes 28311552 | tf_op jit(solution)/shard_map/all_gather | solution.py:305
  29.7 168.9 %collective-permute-start.4 = (bf16[2,1536,1024]{2,1,0:T(8,128)(2,1)}, bf16[2,1536,1024]{2,1,0:T(8,128)(2,1)}, u32[]{:S(2)}, u32[]{:S(2)}) collective-permute-start(bf16[2,1536,1024]{2,1,0:T(8,128)(2,1)} %copy-done), channel_id=1, source_target_pairs={{0,1},{1,0},{2,3},{3,2},{4,5},{5,4},{6,7},{7,6},{8,9},{9,8},{10,11... | collective-permute-start | bytes 18874376 | tf_op jit(solution)/shard_map/ppermute | solution.py:310
  30.6 157.8 %collective-permute-start = (bf16[2,1536,1024]{2,1,0:T(8,128)(2,1)}, bf16[2,1536,1024]{2,1,0:T(8,128)(2,1)}, u32[]{:S(2)}, u32[]{:S(2)}) collective-permute-start(bf16[2,1536,1024]{2,1,0:T(8,128)(2,1)} %copy-done), channel_id=1, source_target_pairs={{0,2},{1,3},{2,0},{3,1},{4,6},{5,7},{6,4},{7,5},{8,10},{9,11},{10,... | collective-permute-start | bytes 18874376 | tf_op jit(solution)/shard_map/ppermute | solution.py:309
  37.2 119.4 %copy-start.2 = (f32[32,2048]{1,0:T(8,128)}, f32[32,2048]{1,0:T(8,128)S(1)}, u32[]{:S(2)}) copy-start(f32[32,2048]{1,0:T(8,128)S(1)} %get-tuple-element.103) | copy-start | bytes 786436
  37.2 119.4 %copy-start.6 = (f32[2048]{0:T(1024)}, f32[2048]{0:T(1024)S(1)}, u32[]{:S(2)}) copy-start(f32[2048]{0:T(1024)S(1)} %get-tuple-element.102) | copy-start | bytes 24580
  37.2 5.3 copy-start.24
  37.5 119.1 %copy-start.8 = (s32[1,2048]{1,0:T(1,128)}, s32[1,2048]{1,0:T(1,128)S(1)}, u32[]{:S(2)}) copy-start(s32[1,2048]{1,0:T(1,128)S(1)} %get-tuple-element.86) | copy-start | bytes 24580
  37.5 119.1 %copy-start.10 = (s32[1,2048]{1,0:T(1,128)}, s32[1,2048]{1,0:T(1,128)S(1)}, u32[]{:S(2)}) copy-start(s32[1,2048]{1,0:T(1,128)S(1)} %get-tuple-element.87) | copy-start | bytes 24580
  37.5 119.1 %copy-start.12 = (s32[1,2048]{1,0:T(1,128)}, s32[1,2048]{1,0:T(1,128)S(1)}, u32[]{:S(2)}) copy-start(s32[1,2048]{1,0:T(1,128)S(1)} %get-tuple-element.88) | copy-start | bytes 24580
  37.5 119.1 %copy-start.14 = (s32[1,2048]{1,0:T(1,128)}, s32[1,2048]{1,0:T(1,128)S(1)}, u32[]{:S(2)}) copy-start(s32[1,2048]{1,0:T(1,128)S(1)} %get-tuple-element.89) | copy-start | bytes 24580
  37.5 119.1 %copy-start.16 = (s32[1,2048]{1,0:T(1,128)}, s32[1,2048]{1,0:T(1,128)S(1)}, u32[]{:S(2)}) copy-start(s32[1,2048]{1,0:T(1,128)S(1)} %get-tuple-element.90) | copy-start | bytes 24580
  37.5 119.1 %copy-start.18 = (s32[1,2048]{1,0:T(1,128)}, s32[1,2048]{1,0:T(1,128)S(1)}, u32[]{:S(2)}) copy-start(s32[1,2048]{1,0:T(1,128)S(1)} %get-tuple-element.91) | copy-start | bytes 24580
  37.5 119.1 %copy-start.20 = (s32[1,2048]{1,0:T(1,128)}, s32[1,2048]{1,0:T(1,128)S(1)}, u32[]{:S(2)}) copy-start(s32[1,2048]{1,0:T(1,128)S(1)} %get-tuple-element.92) | copy-start | bytes 24580
  37.5 119.1 %copy-start.22 = (s32[1,2048]{1,0:T(1,128)}, s32[1,2048]{1,0:T(1,128)S(1)}, u32[]{:S(2)}) copy-start(s32[1,2048]{1,0:T(1,128)S(1)} %get-tuple-element.93) | copy-start | bytes 24580
  37.9 4.6 copy-start.26
  38.6 134.3 %all-to-all-start.1 = ((f32[16,1,64]{2,1,0:T(1,128)}), f32[16,1,64]{2,1,0:T(1,128)S(1)}, u32[]{:S(2)}, u32[]{:S(2)}) async-start(f32[16,1,64]{2,1,0:T(1,128)} %broadcast_in_dim.89), calls=%async_computation.1 | async-start | bytes 16384 | tf_op jit(solution)/shard_map/all_to_all | solution.py:304
  42.5 114.1 %copy-start.30 = (f32[2048]{0:T(1024)}, f32[2048]{0:T(1024)S(1)}, u32[]{:S(2)}) copy-start(f32[2048]{0:T(1024)S(1)} %multiply.8) | copy-start | bytes 24580
  43.5 133.7 %copy-start.33 = (s32[6]{0:T(128)}, s32[6]{0:T(128)S(1)}, u32[]{:S(2)}) copy-start(s32[6]{0:T(128)S(1)} %fusion.27.src_ref) | copy-start | bytes 76
  152.4 287.4 %collective-permute-start.1 = (bf16[4,1536,1024]{2,1,0:T(8,128)(2,1)}, bf16[4,1536,1024]{2,1,0:T(8,128)(2,1)}, u32[]{:S(2)}, u32[]{:S(2)}) collective-permute-start(bf16[4,1536,1024]{2,1,0:T(8,128)(2,1)} %constant_dynamic-slice_fusion), channel_id=1, source_target_pairs={{0,2},{1,3},{2,0},{3,1},{4,6},{5,7},{6,4},{7,5},{8,10},{9,11},{10,... | collective-permute-start | bytes 37748744 | tf_op jit(solution)/shard_map/ppermute | solution.py:317
  172.9 13.5 %all-to-all-start = ((f32[8,4,2048]{2,1,0:T(4,128)}), f32[8,4,2048]{2,1,0:T(4,128)S(1)}, u32[]{:S(2)}, u32[]{:S(2)}) async-start(f32[8,4,2048]{2,1,0:T(4,128)} %copy.130), calls=%async_computation | async-start | bytes 524288 | tf_op jit(solution)/shard_map/all_to_all | solution.py:337
  176.3 694.0 %all-gather.6.cloned.1.call-start = ((), (), s32[]{:S(2)}) async-start(), calls=%async_computation.4 | async-start | bytes 28311552 | tf_op jit(solution)/shard_map/all_gather | solution.py:305
  198.0 52.0 %collective-permute-start.3 = (bf16[1,1536,1024]{2,1,0:T(8,128)(2,1)}, bf16[1,1536,1024]{2,1,0:T(8,128)(2,1)}, u32[]{:S(2)}, u32[]{:S(2)}) collective-permute-start(bf16[1,1536,1024]{2,1,0:T(8,128)(2,1)} %slice.202), channel_id=1, source_target_pairs={{0,1},{1,0},{2,3},{3,2},{4,5},{5,4},{6,7},{7,6},{8,9},{9,8},{10,11... | collective-permute-start | bytes 9437192 | tf_op jit(solution)/shard_map/ppermute | solution.py:311
  439.8 280.2 %collective-permute-start.2 = (bf16[4,1536,1024]{2,1,0:T(8,128)(2,1)}, bf16[4,1536,1024]{2,1,0:T(8,128)(2,1)}, u32[]{:S(2)}, u32[]{:S(2)}) collective-permute-start(bf16[4,1536,1024]{2,1,0:T(8,128)(2,1)} %collective-permute-done.1.refs_0_), channel_id=1, source_target_pairs={{0,1},{1,0},{2,3},{3,2},{4,5},{5,4},{6,7},{7,6},{8,9},{9,8},{10,11... | collective-permute-start | bytes 37748744 | tf_op jit(solution)/shard_map/ppermute | solution.py:318
  648.5 334.5 %collective-permute-start.5 = (f32[2,1536,1024]{2,1,0:T(8,128)}, f32[2,1536,1024]{2,1,0:T(8,128)}, u32[]{:S(2)}, u32[]{:S(2)}) collective-permute-start(f32[2,1536,1024]{2,1,0:T(8,128)} %get-tuple-element.52), channel_id=1, source_target_pairs={{0,2},{1,3},{2,0},{3,1},{4,6},{5,7},{6,4},{7,5},{8,10},{9,11},{10,... | collective-permute-start | bytes 37748744 | tf_op jit(solution)/shard_map/ppermute | solution.py:373
  870.3 73.9 %copy-start.7 = (f32[2048]{0:T(1024)S(1)}, f32[2048]{0:T(1024)}, u32[]{:S(2)}) copy-start(f32[2048]{0:T(1024)} %copy-done.6) | copy-start | bytes 24580
  870.3 73.9 %copy-start.9 = (s32[1,2048]{1,0:T(1,128)S(1)}, s32[1,2048]{1,0:T(1,128)}, u32[]{:S(2)}) copy-start(s32[1,2048]{1,0:T(1,128)} %copy-done.8) | copy-start | bytes 24580
  870.3 73.9 %copy-start.11 = (s32[1,2048]{1,0:T(1,128)S(1)}, s32[1,2048]{1,0:T(1,128)}, u32[]{:S(2)}) copy-start(s32[1,2048]{1,0:T(1,128)} %copy-done.10) | copy-start | bytes 24580
  870.3 73.9 %copy-start.13 = (s32[1,2048]{1,0:T(1,128)S(1)}, s32[1,2048]{1,0:T(1,128)}, u32[]{:S(2)}) copy-start(s32[1,2048]{1,0:T(1,128)} %copy-done.12) | copy-start | bytes 24580
  870.3 73.9 %copy-start.15 = (s32[1,2048]{1,0:T(1,128)S(1)}, s32[1,2048]{1,0:T(1,128)}, u32[]{:S(2)}) copy-start(s32[1,2048]{1,0:T(1,128)} %copy-done.14) | copy-start | bytes 24580
  944.1 10.4 %copy-start.3 = (f32[32,2048]{1,0:T(8,128)S(1)}, f32[32,2048]{1,0:T(8,128)}, u32[]{:S(2)}) copy-start(f32[32,2048]{1,0:T(8,128)} %copy-done.2) | copy-start | bytes 786436
  944.1 10.4 %copy-start.4 = (f32[32,1,2048]{2,1,0:T(1,128)S(1)}, f32[32,1,2048]{2,1,0:T(1,128)}, u32[]{:S(2)}) copy-start(f32[32,1,2048]{2,1,0:T(1,128)} %get-tuple-element.50) | copy-start | bytes 786436
  944.1 10.4 %copy-start.17 = (s32[1,2048]{1,0:T(1,128)S(1)}, s32[1,2048]{1,0:T(1,128)}, u32[]{:S(2)}) copy-start(s32[1,2048]{1,0:T(1,128)} %copy-done.16) | copy-start | bytes 24580
  944.1 10.4 %copy-start.19 = (s32[1,2048]{1,0:T(1,128)S(1)}, s32[1,2048]{1,0:T(1,128)}, u32[]{:S(2)}) copy-start(s32[1,2048]{1,0:T(1,128)} %copy-done.18) | copy-start | bytes 24580
  944.2 10.4 %copy-start.21 = (s32[1,2048]{1,0:T(1,128)S(1)}, s32[1,2048]{1,0:T(1,128)}, u32[]{:S(2)}) copy-start(s32[1,2048]{1,0:T(1,128)} %copy-done.20) | copy-start | bytes 24580
  944.2 10.4 %copy-start.23 = (s32[1,2048]{1,0:T(1,128)S(1)}, s32[1,2048]{1,0:T(1,128)}, u32[]{:S(2)}) copy-start(s32[1,2048]{1,0:T(1,128)} %copy-done.22) | copy-start | bytes 24580
  944.2 10.4 %copy-start.25 = (f32[2048]{0:T(1024)S(1)}, f32[2048]{0:T(1024)}, u32[]{:S(2)}) copy-start(f32[2048]{0:T(1024)} %copy-done.24) | copy-start | bytes 24580
  944.2 10.4 %copy-start.27 = (f32[2048]{0:T(1024)S(1)}, f32[2048]{0:T(1024)}, u32[]{:S(2)}) copy-start(f32[2048]{0:T(1024)} %copy-done.26) | copy-start | bytes 24580
  944.2 10.4 %copy-start.29 = (bf16[1024,32]{0,1:T(8,128)(2,1)S(1)}, bf16[1024,32]{0,1:T(8,128)(2,1)}, u32[]{:S(2)}) copy-start(bf16[1024,32]{0,1:T(8,128)(2,1)} %param.8) | copy-start | bytes 196612
  944.2 10.4 %copy-start.32 = (f32[32]{0:T(128)S(1)}, f32[32]{0:T(128)}, u32[]{:S(2)}) copy-start(f32[32]{0:T(128)} %get-tuple-element.98) | copy-start | bytes 388
  951.5 9.3 all-to-all-start.2
  963.3 17.8 %all-to-all-start.3 = ((f32[16,1,2048]{2,1,0:T(1,128)}), f32[16,1,2048]{2,1,0:T(1,128)S(1)}, u32[]{:S(2)}, u32[]{:S(2)}) async-start(f32[16,1,2048]{2,1,0:T(1,128)} %reshape.499), calls=%async_computation.3 | async-start | bytes 262144 | tf_op jit(solution)/shard_map/all_to_all | solution.py:304
Sparse Core Ops, SparseCore 0:
  17.0 124.2 all-gather.7
  143.8 159.8 all-gather.13
  306.1 156.8 all-gather.11
  465.3 122.2 all-gather.9
  589.8 121.4 all-gather.5

commit v3 on v2

--- a/solution.py
+++ b/solution.py
@@ -10,9 +10,8 @@
 
 AUX_COEF = 0.001
 SEG = 512
-WIN = 192
-TILE = 640
-EAGER = True
+WIN = 176
+SMALL, TILE = 512, 640
 F32, BF16 = jnp.float32, jnp.bfloat16
 
 
@@ -25,53 +24,60 @@
     return pl.multiple_of(start, 16), jnp.maximum((cnt_ref[row, b + 1] - start + WIN - 1) // WIN, 1)
 
 
-def hot_rows(pos_ref, b, start):
-    pos = pos_ref[0, :, b * SEG:(b + 1) * SEG] - start
+def hot_rows(pos_row, b, start):
+    pos = pos_row[:, b * SEG:(b + 1) * SEG] - start
     return lax.broadcasted_iota(jnp.int32, (WIN, SEG), 0) == pos
 
 
-def gather_rows(cnt_ref, row, pos_ref, w_ref, t_ref, xs, dys, ds, n_seg, n_rows):
-    dim = xs.shape[1]
-    end = 0
+def gather_rows(cnt_ref, experts, t_ref, n_seg):
+    dim = experts[0][3].shape[1]
+    ends = [0] * len(experts)
     for b in range(n_seg):
-        first, n_win = window(cnt_ref, row, b)
-
-        def step(c, _, b=b, first=first):
-            start = pl.multiple_of(first + c * WIN, 16)
-            hot = hot_rows(pos_ref, b, start)
-            sel = hot.astype(F32).astype(BF16)
-            tok = slice(b * SEG, (b + 1) * SEG)
-            w_col = jnp.sum(jnp.where(hot, w_ref[0, :, tok], 0.0), axis=1, keepdims=True)
+        spans = [window(cnt_ref, ex[0], b) for ex in experts]
+        tok = slice(b * SEG, (b + 1) * SEG)
+
+        def step(c, _, b=b, spans=spans, tok=tok, eager=False):
+            starts = [pl.multiple_of(first + c * WIN, 16) for first, _ in spans]
+            hots = [hot_rows(ex[1], b, start) for ex, start in zip(experts, starts)]
+            sel = jnp.concatenate([hot.astype(F32).astype(BF16) for hot in hots], axis=0)
             both = mm(sel, t_ref[tok, :])
-            x_new, dy_new = both[:, :dim], both[:, dim:]
-            d_new = w_col * dy_new
-            outs = [(xs, x_new), (ds, d_new)] + ([(dys, dy_new)] if dys is not None else [])
-            for ref, new in outs:
-                new = new.astype(BF16)
-                ref[pl.ds(start + 16, WIN - 16), :] = new[16:]
-                if b == 0:
-                    ref[pl.ds(start, 16), :] = new[:16]
+            for k, ((row, _, w_row, xs, dys, ds, _), start, hot) in enumerate(zip(experts, starts, hots)):
+                rows = slice(k * WIN, (k + 1) * WIN)
+
+                def store(row=row, w_row=w_row, xs=xs, dys=dys, ds=ds, start=start, hot=hot, rows=rows):
+                    x_new, dy_new = both[rows, :dim], both[rows, dim:]
+                    w_col = jnp.sum(jnp.where(hot, w_row[:, tok], 0.0), axis=1, keepdims=True)
+                    outs = [(xs, x_new), (ds, w_col * dy_new)] + ([(dys, dy_new)] if dys is not None else [])
+                    for ref, new in outs:
+                        new = new.astype(BF16)
+                        ref[pl.ds(start + 16, WIN - 16), :] = new[16:]
+                        if b == 0 or not eager:
+                            ref[pl.ds(start, 16), :] = new[:16]
+                        else:
+                            head = lax.broadcasted_iota(jnp.int32, (16, dim), 0) < cnt_ref[row, b] - start
+                            old = ref[pl.ds(start, 16), :].astype(F32)
+                            ref[pl.ds(start, 16), :] = jnp.where(head, old, new[:16].astype(F32)).astype(BF16)
+
+                if eager:
+                    store()
                 else:
-                    old = ref[pl.ds(start, 16), :].astype(F32)
-                    keep = jnp.where(c == 0, 1.0, 0.0)
-                    ref[pl.ds(start, 16), :] = (jnp.where(keep > 0, old, 0.0) + new[:16].astype(F32)).astype(BF16)
+                    pl.when(c < spans[k][1])(store)
             return 0
 
-        if EAGER:
-            step(0, 0)
-        lax.fori_loop(int(EAGER), n_win, step, 0)
-        end = first + n_win * WIN
-
-    def clear(i, _):
-        at = pl.multiple_of(i * 16, 16)
-        zero = jnp.zeros((16, dim), BF16)
-        xs[pl.ds(at, 16), :] = zero
-        ds[pl.ds(at, 16), :] = zero
-        if dys is not None:
-            dys[pl.ds(at, 16), :] = zero
-        return 0
-
-    lax.fori_loop(end // 16, n_rows // 16, clear, 0)
+        step(0, 0, eager=True)
+        lax.fori_loop(1, functools.reduce(jnp.maximum, [n for _, n in spans]), step, 0)
+        ends = [first + n * WIN for first, n in spans]
+
+    for (_, _, _, xs, dys, ds, n_rows), end in zip(experts, ends):
+        def clear(i, _, xs=xs, dys=dys, ds=ds):
+            at = pl.ds(pl.multiple_of(i * 16, 16), 16)
+            zero = jnp.zeros((16, dim), BF16)
+            for ref in (xs, dys, ds):
+                if ref is not None:
+                    ref[at, :] = zero
+            return 0
+
+        lax.fori_loop(end // 16, n_rows // 16, clear, 0)
 
 
 def slot_grads(x, d, w_ref, dim):
@@ -87,7 +93,7 @@
     return h, jnp.concatenate([dg, du], axis=1)
 
 
-def token_kernel(first, counts, id_ref, src_ref, cnt_ref, pos_ref, w_ref, t_ref, *refs):
+def token_kernel(first, counts, id_ref, src_ref, cnt_ref, pos_ref, w_ref, pos2_ref, w2_ref, t_ref, *refs):
     n_src = len(counts)
     wt_refs = refs[:n_src]
     y_in, dx_in, _, _, y_out, dx_out, a_out, order, wt_buf, xs, dys, ds, os, dxs, y_acc, dx_acc, wt_sem, sems = refs[n_src:]
@@ -95,7 +101,7 @@
     last = pl.num_programs(0) - 1
     row = id_ref[i]
     n_seg = t_ref.shape[0] // SEG
-    dim = xs.shape[1]
+    dim = xs.shape[2]
 
     def fetch(step):
         lo = 0
@@ -126,12 +132,30 @@
     def _():
         fetch(i + 1)
 
-    gather_rows(cnt_ref, row, pos_ref, w_ref, t_ref, xs, dys, ds, n_seg, TILE)
+    @pl.when(i % 2 == 0)
+    def _():
+        gather_rows(cnt_ref, [(row, pos_ref[0], w_ref[0], xs.at[0], dys.at[0], ds.at[0], TILE),
+                              (id_ref[i + 1], pos2_ref[0], w2_ref[0], xs.at[1], dys.at[1], ds.at[1], TILE)], t_ref, n_seg)
+
+    xs, dys, ds = xs.at[i % 2], dys.at[i % 2], ds.at[i % 2]
     pltpu.make_async_copy(wt_refs[0].at[0], wt_buf.at[i % 2], wt_sem.at[i % 2]).wait()
     wt = wt_buf.at[pl.ds(i % 2, 1)]
-    h, dgu = slot_grads(xs[:TILE, :], ds[:TILE, :], wt, dim)
-    os[:TILE, :] = mm(h, wt[0, dim:, :]).astype(BF16)
-    dxs[:TILE, :] = mm(dgu, wt[0, :dim, :], 1, 1).astype(BF16)
+
+    def experts_mlp(rows):
+        h, dgu = slot_grads(xs[:rows, :], ds[:rows, :], wt, dim)
+        os[:rows, :] = mm(h, wt[0, dim:, :]).astype(BF16)
+        dxs[:rows, :] = mm(dgu, wt[0, :dim, :], 1, 1).astype(BF16)
+
+    @pl.when(cnt_ref[row, n_seg] <= SMALL)
+    def _():
+        experts_mlp(SMALL)
+        os[SMALL:SMALL + WIN, :] = jnp.zeros((WIN, dim), BF16)
+        dxs[SMALL:SMALL + WIN, :] = jnp.zeros((WIN, dim), BF16)
+
+    @pl.when(cnt_ref[row, n_seg] > SMALL)
+    def _():
+        experts_mlp(TILE)
+
     if not first:
         @pl.when(i == 0)
         def _():
@@ -145,7 +169,7 @@
 
         def step(c, a_row, b=b, start0=start0, tok=tok):
             start = pl.multiple_of(start0 + c * WIN, 16)
-            hot = hot_rows(pos_ref, b, start)
+            hot = hot_rows(pos_ref[0], b, start)
             sel = hot.astype(F32)
             sel_w = jnp.where(hot, w_ref[0, :, tok], 0.0).astype(BF16)
             o_win = os[pl.ds(start, WIN), :]
@@ -154,10 +178,8 @@
             a_col = jnp.sum(o_win.astype(F32) * dys[pl.ds(start, WIN), :].astype(F32), axis=1, keepdims=True)
             return a_row + jnp.sum(jnp.where(hot, a_col, 0.0), axis=0, keepdims=True)
 
-        a_row = jnp.zeros((1, SEG), F32)
-        if EAGER:
-            a_row = step(0, a_row)
-        a_out[0, :, tok] = lax.fori_loop(int(EAGER), n_win, step, a_row)
+        a_row = step(0, jnp.zeros((1, SEG), F32))
+        a_out[0, :, tok] = lax.fori_loop(1, n_win, step, a_row)
         part = pl.ds(b * SEG, SEG)
         done = [pltpu.make_async_copy(y_acc.at[part], y_out.at[part], sems.at[0, b]),
                 pltpu.make_async_copy(dx_acc.at[part], dx_out.at[part], sems.at[1, b])]
@@ -179,18 +201,20 @@
     _, w_rows, dim = wts[0].shape
     n_here, n_src = sum(counts), len(counts)
     row_spec = pl.BlockSpec((1, 1, tok_count), lambda i, ids, *_: (ids[i], 0, 0))
+    next_spec = pl.BlockSpec((1, 1, tok_count), lambda i, ids, *_: (ids[i // 2 * 2 + 1], 0, 0))
     any_spec = pl.BlockSpec(memory_space=pl.ANY)
     acc_shape = jax.ShapeDtypeStruct((tok_count, dim), F32)
-    at = 6 + n_src
+    at = 8 + n_src
     return pl.pallas_call(
         functools.partial(token_kernel, first, counts),
         grid_spec=pltpu.PrefetchScalarGridSpec(
             num_scalar_prefetch=3,
             grid=(n_here,),
-            in_specs=[row_spec, row_spec, pl.BlockSpec(t.shape, lambda i, *_: (0, 0), pipeline_mode=pl.Buffered(1))]
+            in_specs=[row_spec, row_spec, next_spec, next_spec, pl.BlockSpec(t.shape, lambda i, *_: (0, 0), pipeline_mode=pl.Buffered(1))]
             + [any_spec] * (n_src + 4),
             out_specs=[any_spec, any_spec, row_spec, pl.BlockSpec((8, 128), lambda i, *_: (0, 0))],
-            scratch_shapes=[pltpu.VMEM((2, w_rows, dim), BF16)] + [pltpu.VMEM((TILE + WIN, dim), BF16)] * 5
+            scratch_shapes=[pltpu.VMEM((2, w_rows, dim), BF16)] + [pltpu.VMEM((2, TILE + WIN, dim), BF16)] * 3
+            + [pltpu.VMEM((TILE + WIN, dim), BF16)] * 2
             + [pltpu.VMEM((tok_count, dim), F32)] * 2
             + [pltpu.SemaphoreType.DMA((2,)), pltpu.SemaphoreType.DMA((2, tok_count // SEG))],
         ),
@@ -199,14 +223,14 @@
         compiler_params=pltpu.CompilerParams(dimension_semantics=("arbitrary",), vmem_limit_bytes=67000000),
         cost_estimate=pl.CostEstimate(flops=n_here * 2 * 4 * 640 * w_rows * dim, bytes_accessed=50 << 20, transcendentals=0),
         name="token_side",
-    )(ids, srcs, cnt, pos, w, t, *wts, y_in, dx_in, a_in, after)
+    )(ids, srcs, cnt, pos, w, pos, w, t, *wts, y_in, dx_in, a_in, after)
 
 
 def owner_kernel(first, cnt_ref, pos_ref, w_ref, t_ref, wt_ref, acc_in, after, acc_out, order, xs, ds, acc, sem):
     g, e = pl.program_id(0), pl.program_id(1)
     n_grp, n_exp = pl.num_programs(0), pl.num_programs(1)
     n_seg = t_ref.shape[0] // SEG
-    dim = xs.shape[1]
+    dim = xs.shape[2]
     row = g * n_exp + e
 
     @pl.when((g == 0) & (e == 0))
@@ -218,22 +242,33 @@
                 pltpu.make_async_copy(acc_in.at[k], acc.at[k], sem.at[k]).start()
         order[...] = jnp.zeros_like(order)
 
-    n_tile = (cnt_ref[row, n_seg] + TILE - 1) // TILE
-    gather_rows(cnt_ref, row, pos_ref, w_ref, t_ref, xs, None, ds, n_seg, n_tile * TILE)
+    def n_tile(k):
+        return jnp.maximum((cnt_ref[g * n_exp + k, n_seg] + TILE - 1) // TILE, 1)
+
+    @pl.when(e == 0)
+    def _():
+        gather_rows(cnt_ref, [(g * n_exp + k, pos_ref[k], w_ref[k], xs.at[k], None, ds.at[k], n_tile(k) * TILE)
+                              for k in range(xs.shape[0])], t_ref, n_seg)
+
     if not first:
         @pl.when(g == 0)
         def _():
             pltpu.make_async_copy(acc_in.at[e], acc.at[e], sem.at[e]).wait()
 
-    def tile(t, _):
-        at = pl.multiple_of(t * TILE, 16)
-        x, d = xs[pl.ds(at, TILE), :], ds[pl.ds(at, TILE), :]
+    def tile(t, rows=TILE):
+        at = pl.ds(pl.multiple_of(t * rows, 16), rows)
+        x, d = xs[e, at, :], ds[e, at, :]
         h, dgu = slot_grads(x, d, wt_ref, dim)
         acc[e, dim:, :] += mm(h, d, 0, 0)
         acc[e, :dim, :] += mm(x, dgu, 0, 0)
+
+    def large(t, _):
+        tile(t)
         return 0
 
-    lax.fori_loop(0, n_tile, tile, 0)
+    count = cnt_ref[row, n_seg]
+    pl.when(count <= SMALL)(lambda: tile(0, SMALL))
+    lax.fori_loop(0, jnp.where(count <= SMALL, 0, n_tile(e)), large, 0)
 
     @pl.when(g == n_grp - 1)
     def _():
@@ -245,13 +280,13 @@
             pltpu.make_async_copy(acc.at[k], acc_out.at[k], sem.at[k]).wait()
 
 
-def owner_side(first, cnt, pos, w, t, wt, acc, after):
+def owner_side(first, max_rows, cnt, pos, w, t, wt, acc, after):
     n_exp, w_rows, dim = wt.shape
     grp = pos.shape[2]
     n_grp = t.shape[0] // grp
-    per_row = pl.BlockSpec((1, 1, grp), lambda g, e, c: (g * n_exp + e, 0, 0))
+    per_row = pl.BlockSpec((n_exp, 1, grp), lambda g, e, c: (g, 0, 0))
     any_spec = pl.BlockSpec(memory_space=pl.ANY)
-    rows = -(-grp // TILE) * TILE + WIN
+    rows = -(-max_rows // TILE) * TILE + WIN
     return pl.pallas_call(
         functools.partial(owner_kernel, first),
         grid_spec=pltpu.PrefetchScalarGridSpec(
@@ -260,7 +295,7 @@
             in_specs=[per_row, per_row, pl.BlockSpec((grp, t.shape[1]), lambda g, e, c: (g, 0)),
                       pl.BlockSpec((1, w_rows, dim), lambda g, e, c: (e, 0, 0)), any_spec, any_spec],
             out_specs=[any_spec, pl.BlockSpec((8, 128), lambda g, e, c: (0, 0))],
-            scratch_shapes=[pltpu.VMEM((rows, dim), BF16)] * 2
+            scratch_shapes=[pltpu.VMEM((n_exp, rows, dim), BF16)] * 2
             + [pltpu.VMEM((n_exp, w_rows, dim), F32), pltpu.SemaphoreType.DMA((n_exp,))],
         ),
         out_shape=[jax.ShapeDtypeStruct(wt.shape, F32), jax.ShapeDtypeStruct((8, 128), F32)],
@@ -369,7 +404,7 @@
         for c in range(n_half):
             for p, wt in enumerate((wt_nbr, wt_loc)):
                 part = slice((p * n_half + c) * n_row, (p * n_half + c + 1) * n_row)
-                sums[p], order = owner_side(c == 0, own_cnt[part], own_pos[part], own_w[part], t_all[c], wt, sums[p], order)
+                sums[p], order = owner_side(c == 0, min(n_half * capacity, tok_count), own_cnt[part], own_pos[part], own_w[part], t_all[c], wt, sums[p], order)
         from_nbr = lax.ppermute(sums[0], "ep", across)
         half = n_plane // 2
         state = run_token([(odd_nbr, expert(my_core * half + quarter, 1 - my_x, 1), quarter),
@@ -391,9 +426,10 @@
         parts = lax.all_to_all(dw_router.reshape(n_exp, n_dev, dim // n_dev).transpose(1, 0, 2), "ep", 0, 0)
         dw_router = share(jnp.sum(parts, axis=0).T).reshape(dim, n_exp)
         dx_router = lax.dot_general(d_logit, w_router, (((0,), (1,)), ((), ())), preferred_element_type=F32)
-        dw = sums[1] + from_nbr
+        joined = lambda rows, cols: sums[1][:, rows, cols] + from_nbr[:, rows, cols]
+        top, low = slice(0, dim), slice(dim, None)
         return (y_acc.astype(BF16), aux_loss, (dx_acc + dx_router).astype(BF16), dw_router,
-                dw[:, :dim, :ff], dw[:, :dim, ff:], dw[:, dim:])
+                joined(top, slice(0, ff)), joined(top, slice(ff, None)), joined(low, slice(None)))
 
     tok_spec = P("ep")
     return jax.shard_map(

time: 1020 us -> 987 us (0.968)
  Pallas kernels: 642 us -> 613 us
    pallas_call x4, Pallas kernels: 278 us -> 250 us  [owner_side(): pl.pallas_call(functools.partial(owner_kernel, first), grid_spec=pltpu.Pr...]
  transfers between devices with their start and end apart: 15 -> 15, of which waited for: 5 -> 5; matrix products, arithmetic and copies ran while one was open for 8% -> 8% of each run, Pallas kernels for 64% -> 63%
where the time goes in v3:
time: 987 us; the launch traced here: 979 us
  Pallas kernels  613 us (62%)
  waiting for transfers between devices  215 us (22%)
  other arithmetic  51.5 us (5%)
  local copies, waits for them, and re-layouts  47.8 us (5%)
  starting transfers between devices  22.4 us (2%)
  between operations  16.9 us (2%)
  matrix products  12.2 us (1%)
    pallas_call x4, Pallas kernels, token_side(): pl.pallas_call(functools.partial(token_kernel, first, counts), grid_spec=...  363 us
    pallas_call x4, Pallas kernels, owner_side(): pl.pallas_call(functools.partial(owner_kernel, first), grid_spec=pltpu.Pr...  250 us
    ppermute x1, waiting for transfers between devices, local_block(): odd_nbr = lax.ppermute(mine, 'ep', across)  96.5 us
    all_gather x5, waiting for transfers between devices, local_block(): lax.all_gather(a, 'ep', axis=0, tiled=True, axis_index_groups=planes)  95.5 us
  transfers between devices with their start and end apart: 15, of which 5 were waited for; matrix products, arithmetic and copies ran while one was open for 8% of the time, Pallas kernels for 63%

profile of v3, /device:TPU:0, one launch (start us, length us, event | category | flops | bytes accessed | tf_op | source)
XLA Modules:
  0.0 978.5 jit_solution(12142393717614504544)
XLA Ops:
  7.2 3.6 pad_maximum_fusion.refs_0_.wt_ref
  10.9 3.8 fusion.40
  14.7 0.7 copy-done
  15.5 2.8 constant_dynamic-update-slice_fusion.1
  18.3 0.6 copy-done.5
  18.9 0.6 constant_dynamic-update-slice_fusion.t_ref
  19.6 3.8 fusion.39
  23.4 3.5 copy-done.1
  27.0 0.7 all-gather.12.cloned.1.call-update
  28.3 0.9 collective-permute-start.4
  29.1 3.0 collective-permute-start
  32.2 3.5 fusion.42
  36.5 0.6 broadcast_in_dim.89
  37.1 2.8 all-to-all-start.1
  43.2 0.6 pad_add_fusion.1.src_ref
  43.8 0.6 minimum_convert_fusion.cnt_ref
  44.4 95.5 %all-gather.8.cloned.1.call-done.refs_0_ = bf16[8,1536,1024]{2,1,0:T(8,128)(2,1)} async-done(((bf16[1,1536,1024]{2,1,0:T(8,128)(2,1)}), bf16[8,1536,1024]{2,1,0:T(8,128)(2,1)}) %all-gather.8.cloned.1.call-update) | async-done | bytes 25165840 | tf_op jit(solution)/shard_map/all_gather | solution.py:340
  139.9 11.1 %constant_dynamic-slice_fusion = bf16[4,1536,1024]{2,1,0:T(8,128)(2,1)} fusion(bf16[8,1536,1024]{2,1,0:T(8,128)(2,1)} %all-gather.8.cloned.1.call-done.refs_0_, s32[]{:T(128)S(6)} %select_n.123), kind=kLoop, calls=%fused_computation.125 | loop fusion | bytes 25165828 | tf_op jit(solution)/shard_map/dynamic_slice | solution.py:351
  150.9 1.5 collective-permute-start.1
  152.5 2.6 fusion.5.pos_ref.pos2_ref
  156.6 0.9 copy.130
  157.4 14.0 %all-to-all-done.1 = f32[16,1,64]{2,1,0:T(1,128)S(1)} async-done(((f32[16,1,64]{2,1,0:T(1,128)}), f32[16,1,64]{2,1,0:T(1,128)S(1)}, u32[]{:S(2)}, u32[]{:S(2)}) %all-to-all-start.1) | async-done | bytes 4128 | tf_op jit(solution)/shard_map/all_to_all | solution.py:339
  171.4 3.4 all-to-all-start
  175.1 0.7 pad_add_fusion.id_ref
  176.3 0.9 broadcast_in_dim.83.w_ref.w2_ref
  177.2 1.1 slice_multiply_fusion
  179.0 5.9 all-to-all-done
  187.0 3.9 slice.214
  190.9 0.7 copy.138.pos_ref
  191.6 0.7 copy.139.w_ref
  192.4 0.7 copy.140.pos_ref
  193.0 0.7 copy.141.w_ref
  193.7 0.7 copy.142.pos_ref
  194.4 0.7 copy.143.w_ref
  195.1 0.7 copy.144.pos_ref
  195.8 0.7 copy.145.w_ref
  196.5 0.6 fusion.41
  197.1 0.6 broadcast_in_dim.84.refs_2_.refs_3_.refs_5_.acc_in
  197.7 0.8 broadcast_in_dim.85.clone.refs_4_
  198.5 60.0 %token_side.4 = (f32[2048,1024]{1,0:T(8,128)}, f32[2048,1024]{1,0:T(8,128)}, f32[32,1,2048]{2,1,0:T(1,128)}, f32[8,128]{1,0:T(8,128)}) custom-call(s32[4]{0:T(128)} %pad_add_fusion.3.id_ref, s32[4]{0:T(128)} %pad_add_fusion.4.src_ref, s32[32,5]{1,0:T(8,128)} %minimum_convert_fusion.cnt_ref, ...), custom_call_target="tpu_custom_call", output_to_operand_aliasing={{2}: (12, {})} | custom-call | flops 32212254720 | bytes 52428800 | tf_op jit(solution)/shard_map/token_side/pallas_call | solution.py:208
  258.6 83.2 %token_side.5 = (f32[2048,1024]{1,0:T(8,128)}, f32[2048,1024]{1,0:T(8,128)}, f32[32,1,2048]{2,1,0:T(1,128)}, f32[8,128]{1,0:T(8,128)}) custom-call(s32[8]{0:T(128)} %pad_add_fusion.2.id_ref, s32[8]{0:T(128)} %concatenate.36.src_ref, s32[32,5]{1,0:T(8,128)} %minimum_convert_fusion.cnt_ref, ...), custom_call_target="tpu_custom_call", output_to_operand_aliasing={{0}: (11, {}), {1}: (12, {}), {2}: (13, {})} | custom-call | flops 64424509440 | bytes 52428800 | tf_op jit(solution)/shard_map/token_side/pallas_call | solution.py:208
  341.8 96.5 %collective-permute-done.1.refs_0_ = bf16[4,1536,1024]{2,1,0:T(8,128)(2,1)} collective-permute-done((bf16[4,1536,1024]{2,1,0:T(8,128)(2,1)}, bf16[4,1536,1024]{2,1,0:T(8,128)(2,1)}, u32[]{:S(2)}, u32[]{:S(2)}) %collective-permute-start.1) | collective-permute-done | bytes 12582944 | tf_op jit(solution)/shard_map/ppermute | solution.py:352
  438.3 61.5 %owner_side.4 = (f32[2,1536,1024]{2,1,0:T(8,128)}, f32[8,128]{1,0:T(8,128)}) custom-call(s32[8,5]{1,0:T(8,128)} %get-tuple-element.95.cnt_ref, s32[8,1,2048]{2,1,0:T(1,128)} %copy.138.pos_ref, f32[8,1,2048]{2,1,0:T(1,128)} %copy.139.w_ref, bf16[8192,2048]{1,0:T(8,128)(2,1)} %all-gather.14.cloned.1.call-done.t_ref, ...), custom_call_target="tpu_custom_call" | custom-call | flops 64424509440 | bytes 52428800 | tf_op jit(solution)/shard_map/owner_side/pallas_call | solution.py:290
  499.8 64.2 %owner_side.5 = (f32[2,1536,1024]{2,1,0:T(8,128)}, f32[8,128]{1,0:T(8,128)}) custom-call(s32[8,5]{1,0:T(8,128)} %get-tuple-element.96.cnt_ref, s32[8,1,2048]{2,1,0:T(1,128)} %copy.140.pos_ref, f32[8,1,2048]{2,1,0:T(1,128)} %copy.141.w_ref, bf16[8192,2048]{1,0:T(8,128)(2,1)} %all-gather.14.cloned.1.call-done.t_ref, bf16[2,1536,1024]{2,1,0:T(8,128)(2,1)} %copy-done, ...), custom_call_target="tpu_custom_call" | custom-call | flops 64424509440 | bytes 52428800 | tf_op jit(solution)/shard_map/owner_side/pallas_call | solution.py:290
  564.0 63.1 %owner_side.6 = (f32[2,1536,1024]{2,1,0:T(8,128)}, f32[8,128]{1,0:T(8,128)}) custom-call(s32[8,5]{1,0:T(8,128)} %get-tuple-element.94.cnt_ref, s32[8,1,2048]{2,1,0:T(1,128)} %copy.142.pos_ref, f32[8,1,2048]{2,1,0:T(1,128)} %copy.143.w_ref, bf16[8192,2048]{1,0:T(8,128)(2,1)} %all-gather.12.cloned.1.call-done.t_ref, ...), custom_call_target="tpu_custom_call", output_to_operand_aliasing={{0}: (5, {})} | custom-call | flops 64424509440 | bytes 52428800 | tf_op jit(solution)/shard_map/owner_side/pallas_call | solution.py:290
  627.2 61.1 %owner_side.7 = (f32[2,1536,1024]{2,1,0:T(8,128)}, f32[8,128]{1,0:T(8,128)}) custom-call(s32[8,5]{1,0:T(8,128)} %get-tuple-element.97.cnt_ref, s32[8,1,2048]{2,1,0:T(1,128)} %copy.144.pos_ref, f32[8,1,2048]{2,1,0:T(1,128)} %copy.145.w_ref, bf16[8192,2048]{1,0:T(8,128)(2,1)} %all-gather.12.cloned.1.call-done.t_ref, ...), custom_call_target="tpu_custom_call", output_to_operand_aliasing={{0}: (5, {})} | custom-call | flops 64424509440 | bytes 52428800 | tf_op jit(solution)/shard_map/owner_side/pallas_call | solution.py:290
  688.4 152.0 %token_side.6 = (f32[2048,1024]{1,0:T(8,128)}, f32[2048,1024]{1,0:T(8,128)}, f32[32,1,2048]{2,1,0:T(1,128)}, f32[8,128]{1,0:T(8,128)}) custom-call(s32[14]{0:T(128)} %pad_add_fusion.id_ref, s32[14]{0:T(128)} %pad_add_fusion.1.src_ref, s32[32,5]{1,0:T(8,128)} %minimum_convert_fusion.cnt_ref, ...), custom_call_target="tpu_custom_call", output_to_operand_aliasing={{0}: (11, {}), {1}: (12, {}), {2}: (13, {})} | custom-call | flops 112742891520 | bytes 52428800 | tf_op jit(solution)/shard_map/token_side/pallas_call | solution.py:208
  840.5 67.7 %token_side.7 = (f32[2048,1024]{1,0:T(8,128)}, f32[2048,1024]{1,0:T(8,128)}, f32[32,1,2048]{2,1,0:T(1,128)}, f32[8,128]{1,0:T(8,128)}) custom-call(s32[6]{0:T(128)} %add_multiply_fusion.1.id_ref, s32[6]{0:T(128)} %copy-done.33, s32[32,5]{1,0:T(8,128)} %minimum_convert_fusion.cnt_ref, ...), custom_call_target="tpu_custom_call", output_to_operand_aliasing={{0}: (9, {}), {1}: (10, {}), {2}: (11, {})} | custom-call | flops 48318382080 | bytes 52428800 | tf_op jit(solution)/shard_map/token_side/pallas_call | solution.py:208
  908.4 1.5 fusion.1
  909.9 1.4 multiply_reduce_fusion
  911.3 3.4 fusion.36
  914.9 0.8 reshape.497
  915.7 8.0 all-to-all-start.2
  923.8 4.8 fusion.37
  928.5 1.4 all-to-all-done.2
  930.5 0.9 reduce.33
  931.6 0.8 reshape.499
  932.4 2.4 all-to-all-start.3
  934.8 9.3 add_convert_fusion
  944.1 6.1 convert_element_type.59
  950.2 1.0 reduce.34
  951.4 0.8 reshape.451
  952.2 6.8 slice_add_fusion
  959.1 11.4 %slice_add_fusion.1 = (f32[2,1024,512]{2,1,0:T(8,128)}, f32[2,1024,512]{2,1,0:T(8,128)}) fusion(f32[2,1536,1024]{2,1,0:T(8,128)} %collective-permute-done.5, f32[2,1536,1024]{2,1,0:T(8,128)} %get-tuple-element.51), kind=kLoop, calls=%fused_computation.3 | loop fusion | flops 2097152 | bytes 25165824 | tf_op jit(solution)/shard_map/add | solution.py:429
  (155 shorter events, 10.2 us)
Async XLA Ops:
  7.2 132.7 %all-gather.8.cloned.1.call-start = ((), (), s32[]{:S(2)}) async-start(), calls=%async_computation.5 | async-start | bytes 28311552 | tf_op jit(solution)/shard_map/all_gather | solution.py:340
  10.9 4.6 copy-start
  15.4 422.9 %all-gather.14.cloned.1.call-start = ((), (), s32[]{:S(2)}) async-start(), calls=%async_computation.8 | async-start | bytes 37748736 | tf_op jit(solution)/shard_map/all_gather | solution.py:340
  15.5 3.5 copy-start.5
  19.6 7.3 copy-start.1
  26.9 5.2 copy-start.28
  26.9 8.9 copy-start.31
  26.9 537.1 %all-gather.12.cloned.1.call-start = ((), (), s32[]{:S(2)}) async-start(), calls=%async_computation.7 | async-start | bytes 37748736 | tf_op jit(solution)/shard_map/all_gather | solution.py:340
  27.7 660.7 %all-gather.10.cloned.1.call-start = ((), (), s32[]{:S(2)}) async-start(), calls=%async_computation.6 | async-start | bytes 28311552 | tf_op jit(solution)/shard_map/all_gather | solution.py:340
  28.3 168.9 %collective-permute-start.4 = (bf16[2,1536,1024]{2,1,0:T(8,128)(2,1)}, bf16[2,1536,1024]{2,1,0:T(8,128)(2,1)}, u32[]{:S(2)}, u32[]{:S(2)}) collective-permute-start(bf16[2,1536,1024]{2,1,0:T(8,128)(2,1)} %copy-done), channel_id=1, source_target_pairs={{0,1},{1,0},{2,3},{3,2},{4,5},{5,4},{6,7},{7,6},{8,9},{9,8},{10,11... | collective-permute-start | bytes 18874376 | tf_op jit(solution)/shard_map/ppermute | solution.py:345
  29.1 157.8 %collective-permute-start = (bf16[2,1536,1024]{2,1,0:T(8,128)(2,1)}, bf16[2,1536,1024]{2,1,0:T(8,128)(2,1)}, u32[]{:S(2)}, u32[]{:S(2)}) collective-permute-start(bf16[2,1536,1024]{2,1,0:T(8,128)(2,1)} %copy-done), channel_id=1, source_target_pairs={{0,2},{1,3},{2,0},{3,1},{4,6},{5,7},{6,4},{7,5},{8,10},{9,11},{10,... | collective-permute-start | bytes 18874376 | tf_op jit(solution)/shard_map/ppermute | solution.py:344
  35.7 119.4 %copy-start.2 = (f32[32,2048]{1,0:T(8,128)}, f32[32,2048]{1,0:T(8,128)S(1)}, u32[]{:S(2)}) copy-start(f32[32,2048]{1,0:T(8,128)S(1)} %get-tuple-element.103) | copy-start | bytes 786436
  35.7 119.4 %copy-start.6 = (f32[2048]{0:T(1024)}, f32[2048]{0:T(1024)S(1)}, u32[]{:S(2)}) copy-start(f32[2048]{0:T(1024)S(1)} %get-tuple-element.102) | copy-start | bytes 24580
  35.8 5.3 copy-start.24
  36.0 119.1 %copy-start.8 = (s32[1,2048]{1,0:T(1,128)}, s32[1,2048]{1,0:T(1,128)S(1)}, u32[]{:S(2)}) copy-start(s32[1,2048]{1,0:T(1,128)S(1)} %get-tuple-element.86) | copy-start | bytes 24580
  36.0 119.1 %copy-start.10 = (s32[1,2048]{1,0:T(1,128)}, s32[1,2048]{1,0:T(1,128)S(1)}, u32[]{:S(2)}) copy-start(s32[1,2048]{1,0:T(1,128)S(1)} %get-tuple-element.87) | copy-start | bytes 24580
  36.0 119.1 %copy-start.12 = (s32[1,2048]{1,0:T(1,128)}, s32[1,2048]{1,0:T(1,128)S(1)}, u32[]{:S(2)}) copy-start(s32[1,2048]{1,0:T(1,128)S(1)} %get-tuple-element.88) | copy-start | bytes 24580
  36.0 119.1 %copy-start.14 = (s32[1,2048]{1,0:T(1,128)}, s32[1,2048]{1,0:T(1,128)S(1)}, u32[]{:S(2)}) copy-start(s32[1,2048]{1,0:T(1,128)S(1)} %get-tuple-element.89) | copy-start | bytes 24580
  36.0 119.1 %copy-start.16 = (s32[1,2048]{1,0:T(1,128)}, s32[1,2048]{1,0:T(1,128)S(1)}, u32[]{:S(2)}) copy-start(s32[1,2048]{1,0:T(1,128)S(1)} %get-tuple-element.90) | copy-start | bytes 24580
  36.0 119.1 %copy-start.18 = (s32[1,2048]{1,0:T(1,128)}, s32[1,2048]{1,0:T(1,128)S(1)}, u32[]{:S(2)}) copy-start(s32[1,2048]{1,0:T(1,128)S(1)} %get-tuple-element.91) | copy-start | bytes 24580
  36.1 119.1 %copy-start.20 = (s32[1,2048]{1,0:T(1,128)}, s32[1,2048]{1,0:T(1,128)S(1)}, u32[]{:S(2)}) copy-start(s32[1,2048]{1,0:T(1,128)S(1)} %get-tuple-element.92) | copy-start | bytes 24580
  36.1 119.1 %copy-start.22 = (s32[1,2048]{1,0:T(1,128)}, s32[1,2048]{1,0:T(1,128)S(1)}, u32[]{:S(2)}) copy-start(s32[1,2048]{1,0:T(1,128)S(1)} %get-tuple-element.93) | copy-start | bytes 24580
  36.5 4.6 copy-start.26
  37.1 134.3 %all-to-all-start.1 = ((f32[16,1,64]{2,1,0:T(1,128)}), f32[16,1,64]{2,1,0:T(1,128)S(1)}, u32[]{:S(2)}, u32[]{:S(2)}) async-start(f32[16,1,64]{2,1,0:T(1,128)} %broadcast_in_dim.89), calls=%async_computation.1 | async-start | bytes 16384 | tf_op jit(solution)/shard_map/all_to_all | solution.py:339
  41.1 114.1 %copy-start.30 = (f32[2048]{0:T(1024)}, f32[2048]{0:T(1024)S(1)}, u32[]{:S(2)}) copy-start(f32[2048]{0:T(1024)S(1)} %multiply.8) | copy-start | bytes 24580
  42.0 133.8 %copy-start.33 = (s32[6]{0:T(128)}, s32[6]{0:T(128)S(1)}, u32[]{:S(2)}) copy-start(s32[6]{0:T(128)S(1)} %fusion.27.src_ref) | copy-start | bytes 76
  150.9 287.4 %collective-permute-start.1 = (bf16[4,1536,1024]{2,1,0:T(8,128)(2,1)}, bf16[4,1536,1024]{2,1,0:T(8,128)(2,1)}, u32[]{:S(2)}, u32[]{:S(2)}) collective-permute-start(bf16[4,1536,1024]{2,1,0:T(8,128)(2,1)} %constant_dynamic-slice_fusion), channel_id=1, source_target_pairs={{0,2},{1,3},{2,0},{3,1},{4,6},{5,7},{6,4},{7,5},{8,10},{9,11},{10,... | collective-permute-start | bytes 37748744 | tf_op jit(solution)/shard_map/ppermute | solution.py:352
  171.4 13.5 %all-to-all-start = ((f32[8,4,2048]{2,1,0:T(4,128)}), f32[8,4,2048]{2,1,0:T(4,128)S(1)}, u32[]{:S(2)}, u32[]{:S(2)}) async-start(f32[8,4,2048]{2,1,0:T(4,128)} %copy.130), calls=%async_computation | async-start | bytes 524288 | tf_op jit(solution)/shard_map/all_to_all | solution.py:372
  174.8 665.6 %all-gather.6.cloned.1.call-start = ((), (), s32[]{:S(2)}) async-start(), calls=%async_computation.4 | async-start | bytes 28311552 | tf_op jit(solution)/shard_map/all_gather | solution.py:340
  196.5 62.1 %collective-permute-start.3 = (bf16[1,1536,1024]{2,1,0:T(8,128)(2,1)}, bf16[1,1536,1024]{2,1,0:T(8,128)(2,1)}, u32[]{:S(2)}, u32[]{:S(2)}) collective-permute-start(bf16[1,1536,1024]{2,1,0:T(8,128)(2,1)} %slice.214), channel_id=1, source_target_pairs={{0,1},{1,0},{2,3},{3,2},{4,5},{5,4},{6,7},{7,6},{8,9},{9,8},{10,11... | collective-permute-start | bytes 9437192 | tf_op jit(solution)/shard_map/ppermute | solution.py:346
  438.3 250.1 %collective-permute-start.2 = (bf16[4,1536,1024]{2,1,0:T(8,128)(2,1)}, bf16[4,1536,1024]{2,1,0:T(8,128)(2,1)}, u32[]{:S(2)}, u32[]{:S(2)}) collective-permute-start(bf16[4,1536,1024]{2,1,0:T(8,128)(2,1)} %collective-permute-done.1.refs_0_), channel_id=1, source_target_pairs={{0,1},{1,0},{2,3},{3,2},{4,5},{5,4},{6,7},{7,6},{8,9},{9,8},{10,11... | collective-permute-start | bytes 37748744 | tf_op jit(solution)/shard_map/ppermute | solution.py:353
  627.2 325.0 %collective-permute-start.5 = (f32[2,1536,1024]{2,1,0:T(8,128)}, f32[2,1536,1024]{2,1,0:T(8,128)}, u32[]{:S(2)}, u32[]{:S(2)}) collective-permute-start(f32[2,1536,1024]{2,1,0:T(8,128)} %get-tuple-element.52), channel_id=1, source_target_pairs={{0,2},{1,3},{2,0},{3,1},{4,6},{5,7},{6,4},{7,5},{8,10},{9,11},{10,... | collective-permute-start | bytes 37748744 | tf_op jit(solution)/shard_map/ppermute | solution.py:408
  840.5 67.9 %copy-start.7 = (f32[2048]{0:T(1024)S(1)}, f32[2048]{0:T(1024)}, u32[]{:S(2)}) copy-start(f32[2048]{0:T(1024)} %copy-done.6) | copy-start | bytes 24580
  840.5 67.9 %copy-start.9 = (s32[1,2048]{1,0:T(1,128)S(1)}, s32[1,2048]{1,0:T(1,128)}, u32[]{:S(2)}) copy-start(s32[1,2048]{1,0:T(1,128)} %copy-done.8) | copy-start | bytes 24580
  840.5 67.9 %copy-start.11 = (s32[1,2048]{1,0:T(1,128)S(1)}, s32[1,2048]{1,0:T(1,128)}, u32[]{:S(2)}) copy-start(s32[1,2048]{1,0:T(1,128)} %copy-done.10) | copy-start | bytes 24580
  840.5 67.9 %copy-start.13 = (s32[1,2048]{1,0:T(1,128)S(1)}, s32[1,2048]{1,0:T(1,128)}, u32[]{:S(2)}) copy-start(s32[1,2048]{1,0:T(1,128)} %copy-done.12) | copy-start | bytes 24580
  840.5 67.9 %copy-start.15 = (s32[1,2048]{1,0:T(1,128)S(1)}, s32[1,2048]{1,0:T(1,128)}, u32[]{:S(2)}) copy-start(s32[1,2048]{1,0:T(1,128)} %copy-done.14) | copy-start | bytes 24580
  908.3 15.4 %copy-start.3 = (f32[32,2048]{1,0:T(8,128)S(1)}, f32[32,2048]{1,0:T(8,128)}, u32[]{:S(2)}) copy-start(f32[32,2048]{1,0:T(8,128)} %copy-done.2) | copy-start | bytes 786436
  908.3 15.4 %copy-start.4 = (f32[32,1,2048]{2,1,0:T(1,128)S(1)}, f32[32,1,2048]{2,1,0:T(1,128)}, u32[]{:S(2)}) copy-start(f32[32,1,2048]{2,1,0:T(1,128)} %get-tuple-element.50) | copy-start | bytes 786436
  908.3 15.4 %copy-start.17 = (s32[1,2048]{1,0:T(1,128)S(1)}, s32[1,2048]{1,0:T(1,128)}, u32[]{:S(2)}) copy-start(s32[1,2048]{1,0:T(1,128)} %copy-done.16) | copy-start | bytes 24580
  908.3 15.4 %copy-start.19 = (s32[1,2048]{1,0:T(1,128)S(1)}, s32[1,2048]{1,0:T(1,128)}, u32[]{:S(2)}) copy-start(s32[1,2048]{1,0:T(1,128)} %copy-done.18) | copy-start | bytes 24580
  908.3 15.4 %copy-start.21 = (s32[1,2048]{1,0:T(1,128)S(1)}, s32[1,2048]{1,0:T(1,128)}, u32[]{:S(2)}) copy-start(s32[1,2048]{1,0:T(1,128)} %copy-done.20) | copy-start | bytes 24580
  908.3 15.4 %copy-start.23 = (s32[1,2048]{1,0:T(1,128)S(1)}, s32[1,2048]{1,0:T(1,128)}, u32[]{:S(2)}) copy-start(s32[1,2048]{1,0:T(1,128)} %copy-done.22) | copy-start | bytes 24580
  908.4 15.4 %copy-start.25 = (f32[2048]{0:T(1024)S(1)}, f32[2048]{0:T(1024)}, u32[]{:S(2)}) copy-start(f32[2048]{0:T(1024)} %copy-done.24) | copy-start | bytes 24580
  908.4 15.4 %copy-start.27 = (f32[2048]{0:T(1024)S(1)}, f32[2048]{0:T(1024)}, u32[]{:S(2)}) copy-start(f32[2048]{0:T(1024)} %copy-done.26) | copy-start | bytes 24580
  908.4 15.4 %copy-start.29 = (bf16[1024,32]{0,1:T(8,128)(2,1)S(1)}, bf16[1024,32]{0,1:T(8,128)(2,1)}, u32[]{:S(2)}) copy-start(bf16[1024,32]{0,1:T(8,128)(2,1)} %param.8) | copy-start | bytes 196612
  908.4 15.4 %copy-start.32 = (f32[32]{0:T(128)S(1)}, f32[32]{0:T(128)}, u32[]{:S(2)}) copy-start(f32[32]{0:T(128)} %get-tuple-element.98) | copy-start | bytes 388
  915.7 14.3 %all-to-all-start.2 = ((f32[16,1,2048]{2,1,0:T(1,128)}), f32[16,1,2048]{2,1,0:T(1,128)S(1)}, u32[]{:S(2)}, u32[]{:S(2)}) async-start(f32[16,1,2048]{2,1,0:T(1,128)} %reshape.497), calls=%async_computation.2 | async-start | bytes 262144 | tf_op jit(solution)/shard_map/all_to_all | solution.py:426
  932.4 17.8 %all-to-all-start.3 = ((f32[16,1,2048]{2,1,0:T(1,128)}), f32[16,1,2048]{2,1,0:T(1,128)S(1)}, u32[]{:S(2)}, u32[]{:S(2)}) async-start(f32[16,1,2048]{2,1,0:T(1,128)} %reshape.499), calls=%async_computation.3 | async-start | bytes 262144 | tf_op jit(solution)/shard_map/all_to_all | solution.py:339
Sparse Core Ops, SparseCore 0:
  15.6 124.2 all-gather.7
  142.3 159.7 all-gather.13
  304.5 156.9 all-gather.11
  463.8 122.2 all-gather.9
  588.3 121.4 all-gather.5
